TPU v7x, 16 devices: a 4x2x1 block of a 4x4x8 slice. The times are simulated.
16 devices in a mesh: dp: 2 (over y, z), ctx: 8 (over x, core).
Axes of the slice: x: 4, y: 2, z: 1, core: 2. Of those that a mesh axis runs over, the one named last changes fastest.
The devices are a block of a 4x4x8 slice.
Arguments:
- x_seq: bfloat16 [1024, 2560], P(('dp', 'ctx')), parts along dimension 0
- pos_ids: int32 [1024], P(('dp', 'ctx')), parts along dimension 0
- seg_ids: int32 [1024], P(('dp', 'ctx')), parts along dimension 0
- w_dq: bfloat16 [2560, 768], replicated
- w_uq: bfloat16 [768, 2560], replicated
- w_qr: bfloat16 [768, 1280], replicated
- w_dkv: bfloat16 [2560, 256], replicated
- w_kr: bfloat16 [2560, 32], replicated
- w_uk: bfloat16 [256, 2560], replicated
- w_uv: bfloat16 [256, 2560], replicated
- w_out: bfloat16 [2560, 2560], replicated
- gain_q: bfloat16 [768], replicated
- gain_kv: bfloat16 [256], replicated
Outputs:
- output: bfloat16 [1024, 2560], P(('dp', 'ctx')), parts along dimension 0
There are 2 independent parts. A program takes and returns all parts, laid end to end along the dimension named above; an argument that names none is the same for every part.
All inputs are finite; a program needn't handle non-finite values.
Results may differ from a plain program's by a relative error of at most 0.00791805.
Values are sent between devices in bfloat16 or wider.
A program may use at most 768 MiB of HBM per device.

v0:
```python
import jax
import jax.numpy as jnp
from jax import lax
from jax.sharding import PartitionSpec as P, NamedSharding

NORM_EPS = 1e-6


def rms_norm(vals, gain):
    mean_sq = jnp.mean(vals * vals, axis=-1, keepdims=True)
    return (vals * lax.rsqrt(mean_sq + NORM_EPS) * gain.astype(jnp.float32)).astype(jnp.bfloat16)


def rope_tables(pos_ids, rope_dim):
    half_dim = rope_dim // 2
    inv_freq = 10000.0 ** (-2.0 * jnp.arange(half_dim, dtype=jnp.float32) / rope_dim)
    angles = pos_ids.astype(jnp.float32)[:, None] * inv_freq[None, :]
    return jnp.cos(angles), jnp.sin(angles)


def apply_rope(vals, cos_tab, sin_tab):
    half_dim = vals.shape[-1] // 2
    lead_half = vals[..., :half_dim]
    tail_half = vals[..., half_dim:]
    return jnp.concatenate([lead_half * cos_tab - tail_half * sin_tab, tail_half * cos_tab + lead_half * sin_tab], axis=-1)


def solution(mesh):
    group_size = mesh.shape['ctx']
    shift_pairs = [(source, (source + 1) % group_size) for source in range(group_size)]
    row_spec = P(('dp', 'ctx'), None)
    id_spec = P(('dp', 'ctx'))

    def per_device(x_rows, pos_rows, seg_rows, w_dq, w_uq, w_qr, w_dkv, w_kr, w_uk, w_uv, w_out, gain_q, gain_kv):
        seq_dev = x_rows.shape[0]
        kv_rank = w_dkv.shape[1]
        rope_dim = w_kr.shape[1]
        num_heads = w_qr.shape[1] // rope_dim
        nope_dim = w_uq.shape[1] // num_heads
        v_dim = w_uv.shape[1] // num_heads
        score_scale = (nope_dim + rope_dim) ** -0.5
        cos_tab, sin_tab = rope_tables(pos_rows, rope_dim)
        c_q = rms_norm(jnp.dot(x_rows, w_dq, preferred_element_type=jnp.float32), gain_q)
        q_nope = jnp.dot(c_q, w_uq, preferred_element_type=jnp.float32).astype(jnp.bfloat16).reshape(seq_dev, num_heads, nope_dim)
        q_rope = jnp.dot(c_q, w_qr, preferred_element_type=jnp.float32).reshape(seq_dev, num_heads, rope_dim)
        q_rope = apply_rope(q_rope, cos_tab[:, None, :], sin_tab[:, None, :]).astype(jnp.bfloat16)
        c_kv = rms_norm(jnp.dot(x_rows, w_dkv, preferred_element_type=jnp.float32), gain_kv)
        k_rope = apply_rope(jnp.dot(x_rows, w_kr, preferred_element_type=jnp.float32), cos_tab, sin_tab).astype(jnp.bfloat16)
        latents = jnp.concatenate([c_kv, k_rope], axis=1)
        key_ids = jnp.stack([pos_rows, seg_rows])
        w_uk3 = w_uk.reshape(kv_rank, num_heads, nope_dim)
        w_uv3 = w_uv.reshape(kv_rank, num_heads, v_dim)

        def attend_block(soft_state, lat_blk, ids_blk):
            run_max, run_sum, run_acc = soft_state
            c_blk = lat_blk[:, :kv_rank]
            k_nope = jnp.einsum('kc,chd->khd', c_blk, w_uk3, preferred_element_type=jnp.float32).astype(jnp.bfloat16)
            v_blk = jnp.einsum('kc,chd->khd', c_blk, w_uv3, preferred_element_type=jnp.float32).astype(jnp.bfloat16)
            scores = jnp.einsum('qhd,khd->qhk', q_nope, k_nope, preferred_element_type=jnp.float32)
            scores = (scores + jnp.einsum('qhr,kr->qhk', q_rope, lat_blk[:, kv_rank:], preferred_element_type=jnp.float32)) * score_scale
            allowed = ((ids_blk[0][None, :] <= pos_rows[:, None]) & (ids_blk[1][None, :] == seg_rows[:, None]))[:, None, :]
            scores = jnp.where(allowed, scores, -1e30)
            new_max = jnp.maximum(run_max, jnp.max(scores, axis=-1))
            weights = jnp.where(allowed, jnp.exp(scores - new_max[..., None]), 0.0)
            rescale = jnp.exp(run_max - new_max)
            run_sum = run_sum * rescale + jnp.sum(weights, axis=-1)
            run_acc = run_acc * rescale[..., None] + jnp.einsum('qhk,khd->qhd', weights.astype(jnp.bfloat16), v_blk, preferred_element_type=jnp.float32)
            return new_max, run_sum, run_acc

        soft_state = (jnp.full((seq_dev, num_heads), -1e30, jnp.float32), jnp.zeros((seq_dev, num_heads), jnp.float32), jnp.zeros((seq_dev, num_heads, v_dim), jnp.float32))
        soft_state = attend_block(soft_state, latents, key_ids)

        def hop_step(hop_index, loop_carry):
            lat_blk, ids_blk, block_state = loop_carry
            lat_blk = lax.ppermute(lat_blk, 'ctx', shift_pairs)
            ids_blk = lax.ppermute(ids_blk, 'ctx', shift_pairs)
            return lat_blk, ids_blk, attend_block(block_state, lat_blk, ids_blk)

        final_carry = lax.fori_loop(1, group_size, hop_step, (latents, key_ids, soft_state))
        _, run_sum, run_acc = final_carry[2]
        attn_out = (run_acc / run_sum[..., None]).astype(jnp.bfloat16).reshape(seq_dev, num_heads * v_dim)
        return jnp.dot(attn_out, w_out, preferred_element_type=jnp.float32).astype(jnp.bfloat16)

    return jax.shard_map(per_device, mesh=mesh, in_specs=(row_spec, id_spec, id_spec) + (P(),) * 10, out_specs=row_spec, check_vma=False)
```

profile of v0, /device:TPU:112, one launch (start us, length us, event | category | flops | bytes accessed | tf_op | source)
XLA Modules:
  0.0 141.2 jit_solution(12637466804030388590)
XLA Ops:
  0.0 3.3 %multiply_reduce_fusion = (f32[64]{0:T(128)S(1)}, f32[64,768]{1,0:T(8,128)S(1)}) fusion(bf16[64,2560]{1,0:T(8,128)(2,1)} %param.15, bf16[2560,768]{1,0:T(8,128)(2,1)} %param.18), kind=kOutput, calls=%fused_computation.43 | convolution fusion | flops 251756480 | bytes 4456704 | tf_op jit(solution)/shard_map/dot_general | solution.py:43
  6.7 2.0 %multiply_reduce_fusion.1 = (f32[64]{0:T(128)S(1)}, f32[64,256]{1,0:T(8,128)S(1)}) fusion(bf16[64,2560]{1,0:T(8,128)(2,1)S(1)} %copy-done.3, bf16[2560,256]{1,0:T(8,128)(2,1)} %param.21), kind=kOutput, calls=%fused_computation.45 | convolution fusion | flops 83918784 | bytes 1704192 | tf_op jit(solution)/shard_map/dot_general | solution.py:47
  8.8 2.4 %copy.46 = bf16[256,2560]{0,1:T(8,128)(2,1)} copy(bf16[256,2560]{1,0:T(8,128)(2,1)} %param.23) | data formatting | bytes 2621440 | tf_op args[8]
  11.3 3.5 %convolution_bitcast_fusion.3 = f32[64,40,64]{0,2,1:T(8,128)} fusion(bf16[256,40,64]{0,2,1:T(8,128)(2,1)} %bitcast.9, bf16[64,256]{1,0:T(8,128)(2,1)S(1)} %multiply_convert_fusion.1, bf16[64,40,64]{2,1,0:T(8,128)(2,1)S(1)} %reshape.189), kind=kOutput, calls=%fused_computation.27 | convolution fusion | flops 105021440 | bytes 2326528 | tf_op jit(solution)/shard_map/qhd,khd->qhk/dot_general | solution.py:59
  15.6 1.9 %fusion.31 = (f32[64,40]{0,1:T(8,128)S(1)}, f32[64,40,64]{0,2,1:T(8,128)S(1)}) fusion(f32[64,40,64]{0,2,1:T(8,128)} %convolution_bitcast_fusion.3, bf16[64,16]{0,1:T(8,128)(2,1)S(1)} %get-tuple-element.144, bf16[64,16]{0,1:T(8,128)(2,1)S(1)} %get-tuple-element.145, bf16[64,40,16]{0,2,1:T(8,128)(2,1)} %get-tuple-element.137, ...), kind=kOutput, calls=%fused_computation.69 | convolution fusion | flops 11474432 | bytes 1492992 | tf_op jit(solution)/shard_map/qhr,kr->qhk/dot_general | solution.py:60
  18.4 2.4 %copy.49 = bf16[256,2560]{0,1:T(8,128)(2,1)} copy(bf16[256,2560]{1,0:T(8,128)(2,1)} %param.24) | data formatting | bytes 2621440 | tf_op args[9]
  20.9 3.3 %fusion.11 = f32[64,40,64]{0,2,1:T(8,128)} fusion(bf16[256,40,64]{0,2,1:T(8,128)(2,1)} %bitcast.13, f32[64,40,64]{0,2,1:T(8,128)S(1)} %get-tuple-element.151, f32[64,40]{0,1:T(8,128)S(1)} %copy-done.5, f32[64,40]{0,1:T(8,128)S(1)} %broadcast_maximum_fusion, pred[64,64]{0,1:T(8,128)(4,1)S(1)} %compare_and_fusion.1, ...), kind=kOutput, calls=%fused_computation.28 | convolution fusion | flops 105676800 | bytes 2678784 | tf_op jit(solution)/shard_map/qhk,khd->qhd/dot_general | solution.py:67
  26.2 2.1 %copy.47 = bf16[64,40,64]{2,0,1:T(8,128)(2,1)} copy(bf16[64,40,64]{2,1,0:T(8,128)(2,1)} %copy-done.1) | data formatting | bytes 655360 | tf_op jit(solution)/shard_map/reshape | solution.py:44
  29.0 102.8 %while.18 = (s32[]{:T(128)}, bf16[64,288]{1,0:T(8,128)(2,1)S(1)}, s32[2,64]{1,0:T(2,128)S(1)}, f32[64,40]{0,1:T(8,128)S(1)}, f32[64,40]{0,1:T(8,128)S(1)}, /*ind...) while((s32[]{:T(128)}, bf16[64,288]{1,0:T(8,128)(2,1)S(1)}, ...), condition=%wide.region_7.8_spmd, body=%wide.region_4.7_spmd.sunk | while | flops 222512128 | bytes 8873165 | solution.py:79
  29.0 2.5 %collective-permute-start = (bf16[64,288]{1,0:T(8,128)(2,1)S(1)}, bf16[64,288]{1,0:T(8,128)(2,1)S(1)}, u32[]{:S(2)}, u32[]{:S(2)}) collective-permute-start(bf16[64,288]{1,0:T(8,128)(2,1)S(1)} %get-tuple-element.251), channel_id=1, source_target_pairs={{0,1},{1,2},{2,3},{3,4},{4,5},{5,6},{6,7},{7,0},{8,9},{9,10},{10,1... | collective-permute-start | bytes 110600 | tf_op jit(solution)/shard_map/while/body/eval_jaxpr/ppermute | solution.py:75
  31.5 2.2 %collective-permute-done.1 = s32[2,64]{1,0:T(2,128)S(1)} collective-permute-done((s32[2,64]{1,0:T(2,128)S(1)}, s32[2,64]{1,0:T(2,128)S(1)}, u32[]{:S(2)}, u32[]{:S(2)}) %collective-permute-start.1) | collective-permute-done | bytes 544 | tf_op jit(solution)/shard_map/while/body/eval_jaxpr/ppermute | solution.py:76
  34.4 3.6 %convolution_bitcast_fusion.5 = f32[64,40,64]{0,2,1:T(8,128)} fusion(bf16[64,40,64]{2,0,1:T(8,128)(2,1)} %get-tuple-element.272, bf16[256,40,64]{0,2,1:T(8,128)(2,1)} %get-tuple-element.271, bf16[64,288]{1,0:T(8,128)(2,1)S(1)} %collective-permute-done), kind=kOutput, calls=%fused_computation.3.clone.1 | convolution fusion | flops 105021440 | bytes 2326528 | tf_op jit(solution)/shard_map/while/body/eval_jaxpr/qhd,khd->qhk/dot_general | solution.py:59
  40.3 3.8 %fusion.64 = f32[64,40,64]{0,2,1:T(8,128)} fusion(f32[64,40,64]{0,2,1:T(8,128)} %get-tuple-element.255, bf16[256,40,64]{0,2,1:T(8,128)(2,1)} %get-tuple-element.274, f32[64,40,64]{0,2,1:T(8,128)S(1)} %get-tuple-element.234, f32[64,40]{0,1:T(8,128)S(1)} %get-tuple-element.236, f32[64,40]{0,1:T(8,128)S(1)} %max.4, ...), kind=kOutput, calls=%fused_computation.4.clone.1 | convolution fusion | flops 105840640 | bytes 4014080 | tf_op jit(solution)/shard_map/while/body/eval_jaxpr/qhk,khd->qhd/dot_general | solution.py:67
  44.9 3.4 %collective-permute-done.1 = s32[2,64]{1,0:T(2,128)S(1)} collective-permute-done((s32[2,64]{1,0:T(2,128)S(1)}, s32[2,64]{1,0:T(2,128)S(1)}, u32[]{:S(2)}, u32[]{:S(2)}) %collective-permute-start.1) | collective-permute-done | bytes 544 | tf_op jit(solution)/shard_map/while/body/eval_jaxpr/ppermute | solution.py:76
  49.0 3.6 %convolution_bitcast_fusion.5 = f32[64,40,64]{0,2,1:T(8,128)} fusion(bf16[64,40,64]{2,0,1:T(8,128)(2,1)} %get-tuple-element.272, bf16[256,40,64]{0,2,1:T(8,128)(2,1)} %get-tuple-element.271, bf16[64,288]{1,0:T(8,128)(2,1)S(1)} %collective-permute-done), kind=kOutput, calls=%fused_computation.3.clone.1 | convolution fusion | flops 105021440 | bytes 2326528 | tf_op jit(solution)/shard_map/while/body/eval_jaxpr/qhd,khd->qhk/dot_general | solution.py:59
  54.9 3.8 %fusion.64 = f32[64,40,64]{0,2,1:T(8,128)} fusion(f32[64,40,64]{0,2,1:T(8,128)} %get-tuple-element.255, bf16[256,40,64]{0,2,1:T(8,128)(2,1)} %get-tuple-element.274, f32[64,40,64]{0,2,1:T(8,128)S(1)} %get-tuple-element.234, f32[64,40]{0,1:T(8,128)S(1)} %get-tuple-element.236, f32[64,40]{0,1:T(8,128)S(1)} %max.4, ...), kind=kOutput, calls=%fused_computation.4.clone.1 | convolution fusion | flops 105840640 | bytes 4014080 | tf_op jit(solution)/shard_map/while/body/eval_jaxpr/qhk,khd->qhd/dot_general | solution.py:67
  58.7 4.2 %collective-permute-done.1 = s32[2,64]{1,0:T(2,128)S(1)} collective-permute-done((s32[2,64]{1,0:T(2,128)S(1)}, s32[2,64]{1,0:T(2,128)S(1)}, u32[]{:S(2)}, u32[]{:S(2)}) %collective-permute-start.1) | collective-permute-done | bytes 544 | tf_op jit(solution)/shard_map/while/body/eval_jaxpr/ppermute | solution.py:76
  63.7 3.6 %convolution_bitcast_fusion.5 = f32[64,40,64]{0,2,1:T(8,128)} fusion(bf16[64,40,64]{2,0,1:T(8,128)(2,1)} %get-tuple-element.272, bf16[256,40,64]{0,2,1:T(8,128)(2,1)} %get-tuple-element.271, bf16[64,288]{1,0:T(8,128)(2,1)S(1)} %collective-permute-done), kind=kOutput, calls=%fused_computation.3.clone.1 | convolution fusion | flops 105021440 | bytes 2326528 | tf_op jit(solution)/shard_map/while/body/eval_jaxpr/qhd,khd->qhk/dot_general | solution.py:59
  69.5 3.8 %fusion.64 = f32[64,40,64]{0,2,1:T(8,128)} fusion(f32[64,40,64]{0,2,1:T(8,128)} %get-tuple-element.255, bf16[256,40,64]{0,2,1:T(8,128)(2,1)} %get-tuple-element.274, f32[64,40,64]{0,2,1:T(8,128)S(1)} %get-tuple-element.234, f32[64,40]{0,1:T(8,128)S(1)} %get-tuple-element.236, f32[64,40]{0,1:T(8,128)S(1)} %max.4, ...), kind=kOutput, calls=%fused_computation.4.clone.1 | convolution fusion | flops 105840640 | bytes 4014080 | tf_op jit(solution)/shard_map/while/body/eval_jaxpr/qhk,khd->qhd/dot_general | solution.py:67
  73.3 4.2 %collective-permute-done.1 = s32[2,64]{1,0:T(2,128)S(1)} collective-permute-done((s32[2,64]{1,0:T(2,128)S(1)}, s32[2,64]{1,0:T(2,128)S(1)}, u32[]{:S(2)}, u32[]{:S(2)}) %collective-permute-start.1) | collective-permute-done | bytes 544 | tf_op jit(solution)/shard_map/while/body/eval_jaxpr/ppermute | solution.py:76
  78.3 3.6 %convolution_bitcast_fusion.5 = f32[64,40,64]{0,2,1:T(8,128)} fusion(bf16[64,40,64]{2,0,1:T(8,128)(2,1)} %get-tuple-element.272, bf16[256,40,64]{0,2,1:T(8,128)(2,1)} %get-tuple-element.271, bf16[64,288]{1,0:T(8,128)(2,1)S(1)} %collective-permute-done), kind=kOutput, calls=%fused_computation.3.clone.1 | convolution fusion | flops 105021440 | bytes 2326528 | tf_op jit(solution)/shard_map/while/body/eval_jaxpr/qhd,khd->qhk/dot_general | solution.py:59
  84.2 3.8 %fusion.64 = f32[64,40,64]{0,2,1:T(8,128)} fusion(f32[64,40,64]{0,2,1:T(8,128)} %get-tuple-element.255, bf16[256,40,64]{0,2,1:T(8,128)(2,1)} %get-tuple-element.274, f32[64,40,64]{0,2,1:T(8,128)S(1)} %get-tuple-element.234, f32[64,40]{0,1:T(8,128)S(1)} %get-tuple-element.236, f32[64,40]{0,1:T(8,128)S(1)} %max.4, ...), kind=kOutput, calls=%fused_computation.4.clone.1 | convolution fusion | flops 105840640 | bytes 4014080 | tf_op jit(solution)/shard_map/while/body/eval_jaxpr/qhk,khd->qhd/dot_general | solution.py:67
  87.9 4.2 %collective-permute-done.1 = s32[2,64]{1,0:T(2,128)S(1)} collective-permute-done((s32[2,64]{1,0:T(2,128)S(1)}, s32[2,64]{1,0:T(2,128)S(1)}, u32[]{:S(2)}, u32[]{:S(2)}) %collective-permute-start.1) | collective-permute-done | bytes 544 | tf_op jit(solution)/shard_map/while/body/eval_jaxpr/ppermute | solution.py:76
  92.9 3.6 %convolution_bitcast_fusion.5 = f32[64,40,64]{0,2,1:T(8,128)} fusion(bf16[64,40,64]{2,0,1:T(8,128)(2,1)} %get-tuple-element.272, bf16[256,40,64]{0,2,1:T(8,128)(2,1)} %get-tuple-element.271, bf16[64,288]{1,0:T(8,128)(2,1)S(1)} %collective-permute-done), kind=kOutput, calls=%fused_computation.3.clone.1 | convolution fusion | flops 105021440 | bytes 2326528 | tf_op jit(solution)/shard_map/while/body/eval_jaxpr/qhd,khd->qhk/dot_general | solution.py:59
  98.8 3.8 %fusion.64 = f32[64,40,64]{0,2,1:T(8,128)} fusion(f32[64,40,64]{0,2,1:T(8,128)} %get-tuple-element.255, bf16[256,40,64]{0,2,1:T(8,128)(2,1)} %get-tuple-element.274, f32[64,40,64]{0,2,1:T(8,128)S(1)} %get-tuple-element.234, f32[64,40]{0,1:T(8,128)S(1)} %get-tuple-element.236, f32[64,40]{0,1:T(8,128)S(1)} %max.4, ...), kind=kOutput, calls=%fused_computation.4.clone.1 | convolution fusion | flops 105840640 | bytes 4014080 | tf_op jit(solution)/shard_map/while/body/eval_jaxpr/qhk,khd->qhd/dot_general | solution.py:67
  102.6 4.2 %collective-permute-done.1 = s32[2,64]{1,0:T(2,128)S(1)} collective-permute-done((s32[2,64]{1,0:T(2,128)S(1)}, s32[2,64]{1,0:T(2,128)S(1)}, u32[]{:S(2)}, u32[]{:S(2)}) %collective-permute-start.1) | collective-permute-done | bytes 544 | tf_op jit(solution)/shard_map/while/body/eval_jaxpr/ppermute | solution.py:76
  107.5 3.6 %convolution_bitcast_fusion.5 = f32[64,40,64]{0,2,1:T(8,128)} fusion(bf16[64,40,64]{2,0,1:T(8,128)(2,1)} %get-tuple-element.272, bf16[256,40,64]{0,2,1:T(8,128)(2,1)} %get-tuple-element.271, bf16[64,288]{1,0:T(8,128)(2,1)S(1)} %collective-permute-done), kind=kOutput, calls=%fused_computation.3.clone.1 | convolution fusion | flops 105021440 | bytes 2326528 | tf_op jit(solution)/shard_map/while/body/eval_jaxpr/qhd,khd->qhk/dot_general | solution.py:59
  113.4 3.8 %fusion.64 = f32[64,40,64]{0,2,1:T(8,128)} fusion(f32[64,40,64]{0,2,1:T(8,128)} %get-tuple-element.255, bf16[256,40,64]{0,2,1:T(8,128)(2,1)} %get-tuple-element.274, f32[64,40,64]{0,2,1:T(8,128)S(1)} %get-tuple-element.234, f32[64,40]{0,1:T(8,128)S(1)} %get-tuple-element.236, f32[64,40]{0,1:T(8,128)S(1)} %max.4, ...), kind=kOutput, calls=%fused_computation.4.clone.1 | convolution fusion | flops 105840640 | bytes 4014080 | tf_op jit(solution)/shard_map/while/body/eval_jaxpr/qhk,khd->qhd/dot_general | solution.py:67
  117.2 4.2 %collective-permute-done.1 = s32[2,64]{1,0:T(2,128)S(1)} collective-permute-done((s32[2,64]{1,0:T(2,128)S(1)}, s32[2,64]{1,0:T(2,128)S(1)}, u32[]{:S(2)}, u32[]{:S(2)}) %collective-permute-start.1) | collective-permute-done | bytes 544 | tf_op jit(solution)/shard_map/while/body/eval_jaxpr/ppermute | solution.py:76
  122.2 3.6 %convolution_bitcast_fusion.5 = f32[64,40,64]{0,2,1:T(8,128)} fusion(bf16[64,40,64]{2,0,1:T(8,128)(2,1)} %get-tuple-element.272, bf16[256,40,64]{0,2,1:T(8,128)(2,1)} %get-tuple-element.271, bf16[64,288]{1,0:T(8,128)(2,1)S(1)} %collective-permute-done), kind=kOutput, calls=%fused_computation.3.clone.1 | convolution fusion | flops 105021440 | bytes 2326528 | tf_op jit(solution)/shard_map/while/body/eval_jaxpr/qhd,khd->qhk/dot_general | solution.py:59
  128.0 3.8 %fusion.64 = f32[64,40,64]{0,2,1:T(8,128)} fusion(f32[64,40,64]{0,2,1:T(8,128)} %get-tuple-element.255, bf16[256,40,64]{0,2,1:T(8,128)(2,1)} %get-tuple-element.274, f32[64,40,64]{0,2,1:T(8,128)S(1)} %get-tuple-element.234, f32[64,40]{0,1:T(8,128)S(1)} %get-tuple-element.236, f32[64,40]{0,1:T(8,128)S(1)} %max.4, ...), kind=kOutput, calls=%fused_computation.4.clone.1 | convolution fusion | flops 105840640 | bytes 4014080 | tf_op jit(solution)/shard_map/while/body/eval_jaxpr/qhk,khd->qhd/dot_general | solution.py:67
  133.3 7.9 %convolution_convert_fusion.2 = bf16[64,2560]{1,0:T(8,128)(2,1)} fusion(bf16[64,2560]{0,1:T(8,128)(2,1)S(1)} %bitcast.81, bf16[2560,2560]{1,0:T(8,128)(2,1)} %param.25), kind=kOutput, calls=%fused_computation.22 | convolution fusion | flops 839024640 | bytes 13762560 | tf_op jit(solution)/shard_map/dot_general | solution.py:82
  (124 shorter events, 30.7 us)
Async XLA Ops:
  0.0 3.3 %copy-start = (bf16[768,1280]{1,0:T(8,128)(2,1)S(1)}, bf16[768,1280]{1,0:T(8,128)(2,1)}, u32[]{:S(2)}) copy-start(bf16[768,1280]{1,0:T(8,128)(2,1)} %param.20) | copy-start | bytes 5898244
  0.0 3.3 %copy-start.7 = (bf16[768]{0:T(1024)(128)(2,1)S(1)}, bf16[768]{0:T(1024)(128)(2,1)}, u32[]{:S(2)}) copy-start(bf16[768]{0:T(1024)(128)(2,1)} %param.26) | copy-start | bytes 4612
  0.0 4.2 %copy-start.3 = (bf16[64,2560]{1,0:T(8,128)(2,1)S(1)}, bf16[64,2560]{1,0:T(8,128)(2,1)}, u32[]{:S(2)}) copy-start(bf16[64,2560]{1,0:T(8,128)(2,1)} %param.15) | copy-start | bytes 983044
  0.0 4.3 %copy-start.4 = (bf16[2560,32]{0,1:T(8,128)(2,1)S(1)}, bf16[2560,32]{0,1:T(8,128)(2,1)}, u32[]{:S(2)}) copy-start(bf16[2560,32]{0,1:T(8,128)(2,1)} %param.22) | copy-start | bytes 491524
  0.0 4.5 %copy-start.6 = (s32[64]{0:T(128)S(1)}, s32[64]{0:T(128)}, u32[]{:S(2)}) copy-start(s32[64]{0:T(128)} %param.16) | copy-start | bytes 772
  3.3 2.1 %copy-start.2 = (bf16[768,2560]{1,0:T(8,128)(2,1)S(1)}, bf16[768,2560]{1,0:T(8,128)(2,1)}, u32[]{:S(2)}) copy-start(bf16[768,2560]{1,0:T(8,128)(2,1)} %param.19) | copy-start | bytes 11796484
  6.3 2.4 %copy-start.8 = (bf16[256]{0:T(256)(128)(2,1)S(1)}, bf16[256]{0:T(256)(128)(2,1)}, u32[]{:S(2)}) copy-start(bf16[256]{0:T(256)(128)(2,1)} %param.27) | copy-start | bytes 1540
  6.7 4.6 %copy-start.1 = (bf16[64,40,64]{2,1,0:T(8,128)(2,1)}, bf16[64,40,64]{2,1,0:T(8,128)(2,1)S(1)}, u32[]{:S(2)}) copy-start(bf16[64,40,64]{2,1,0:T(8,128)(2,1)S(1)} %reshape.189) | copy-start | bytes 983044
  18.4 2.4 %copy-start.5 = (f32[64,40]{0,1:T(8,128)S(1)}, f32[64,40]{0,1:T(8,128)}, u32[]{:S(2)}) copy-start(f32[64,40]{0,1:T(8,128)} %get-tuple-element.138) | copy-start | bytes 30724
  29.0 4.7 %collective-permute-start.1 = (s32[2,64]{1,0:T(2,128)S(1)}, s32[2,64]{1,0:T(2,128)S(1)}, u32[]{:S(2)}, u32[]{:S(2)}) collective-permute-start(s32[2,64]{1,0:T(2,128)S(1)} %get-tuple-element.252), channel_id=1, source_target_pairs={{0,1},{1,2},{2,3},{3,4},{4,5},{5,6},{6,7},{7,0},{8,9},{9,10},{10,1... | collective-permute-start | bytes 1544 | tf_op jit(solution)/shard_map/while/body/eval_jaxpr/ppermute | solution.py:76
  29.0 5.4 %collective-permute-start = (bf16[64,288]{1,0:T(8,128)(2,1)S(1)}, bf16[64,288]{1,0:T(8,128)(2,1)S(1)}, u32[]{:S(2)}, u32[]{:S(2)}) collective-permute-start(bf16[64,288]{1,0:T(8,128)(2,1)S(1)} %get-tuple-element.251), channel_id=1, source_target_pairs={{0,1},{1,2},{2,3},{3,4},{4,5},{5,6},{6,7},{7,0},{8,9},{9,10},{10,1... | collective-permute-start | bytes 110600 | tf_op jit(solution)/shard_map/while/body/eval_jaxpr/ppermute | solution.py:75
  44.1 4.2 %collective-permute-start.1 = (s32[2,64]{1,0:T(2,128)S(1)}, s32[2,64]{1,0:T(2,128)S(1)}, u32[]{:S(2)}, u32[]{:S(2)}) collective-permute-start(s32[2,64]{1,0:T(2,128)S(1)} %get-tuple-element.252), channel_id=1, source_target_pairs={{0,1},{1,2},{2,3},{3,4},{4,5},{5,6},{6,7},{7,0},{8,9},{9,10},{10,1... | collective-permute-start | bytes 1544 | tf_op jit(solution)/shard_map/while/body/eval_jaxpr/ppermute | solution.py:76
  44.1 5.0 %collective-permute-start = (bf16[64,288]{1,0:T(8,128)(2,1)S(1)}, bf16[64,288]{1,0:T(8,128)(2,1)S(1)}, u32[]{:S(2)}, u32[]{:S(2)}) collective-permute-start(bf16[64,288]{1,0:T(8,128)(2,1)S(1)} %get-tuple-element.251), channel_id=1, source_target_pairs={{0,1},{1,2},{2,3},{3,4},{4,5},{5,6},{6,7},{7,0},{8,9},{9,10},{10,1... | collective-permute-start | bytes 110600 | tf_op jit(solution)/shard_map/while/body/eval_jaxpr/ppermute | solution.py:75
  58.7 4.2 %collective-permute-start.1 = (s32[2,64]{1,0:T(2,128)S(1)}, s32[2,64]{1,0:T(2,128)S(1)}, u32[]{:S(2)}, u32[]{:S(2)}) collective-permute-start(s32[2,64]{1,0:T(2,128)S(1)} %get-tuple-element.252), channel_id=1, source_target_pairs={{0,1},{1,2},{2,3},{3,4},{4,5},{5,6},{6,7},{7,0},{8,9},{9,10},{10,1... | collective-permute-start | bytes 1544 | tf_op jit(solution)/shard_map/while/body/eval_jaxpr/ppermute | solution.py:76
  58.7 5.0 %collective-permute-start = (bf16[64,288]{1,0:T(8,128)(2,1)S(1)}, bf16[64,288]{1,0:T(8,128)(2,1)S(1)}, u32[]{:S(2)}, u32[]{:S(2)}) collective-permute-start(bf16[64,288]{1,0:T(8,128)(2,1)S(1)} %get-tuple-element.251), channel_id=1, source_target_pairs={{0,1},{1,2},{2,3},{3,4},{4,5},{5,6},{6,7},{7,0},{8,9},{9,10},{10,1... | collective-permute-start | bytes 110600 | tf_op jit(solution)/shard_map/while/body/eval_jaxpr/ppermute | solution.py:75
  73.3 4.2 %collective-permute-start.1 = (s32[2,64]{1,0:T(2,128)S(1)}, s32[2,64]{1,0:T(2,128)S(1)}, u32[]{:S(2)}, u32[]{:S(2)}) collective-permute-start(s32[2,64]{1,0:T(2,128)S(1)} %get-tuple-element.252), channel_id=1, source_target_pairs={{0,1},{1,2},{2,3},{3,4},{4,5},{5,6},{6,7},{7,0},{8,9},{9,10},{10,1... | collective-permute-start | bytes 1544 | tf_op jit(solution)/shard_map/while/body/eval_jaxpr/ppermute | solution.py:76
  73.3 5.0 %collective-permute-start = (bf16[64,288]{1,0:T(8,128)(2,1)S(1)}, bf16[64,288]{1,0:T(8,128)(2,1)S(1)}, u32[]{:S(2)}, u32[]{:S(2)}) collective-permute-start(bf16[64,288]{1,0:T(8,128)(2,1)S(1)} %get-tuple-element.251), channel_id=1, source_target_pairs={{0,1},{1,2},{2,3},{3,4},{4,5},{5,6},{6,7},{7,0},{8,9},{9,10},{10,1... | collective-permute-start | bytes 110600 | tf_op jit(solution)/shard_map/while/body/eval_jaxpr/ppermute | solution.py:75
  87.9 4.2 %collective-permute-start.1 = (s32[2,64]{1,0:T(2,128)S(1)}, s32[2,64]{1,0:T(2,128)S(1)}, u32[]{:S(2)}, u32[]{:S(2)}) collective-permute-start(s32[2,64]{1,0:T(2,128)S(1)} %get-tuple-element.252), channel_id=1, source_target_pairs={{0,1},{1,2},{2,3},{3,4},{4,5},{5,6},{6,7},{7,0},{8,9},{9,10},{10,1... | collective-permute-start | bytes 1544 | tf_op jit(solution)/shard_map/while/body/eval_jaxpr/ppermute | solution.py:76
  87.9 5.0 %collective-permute-start = (bf16[64,288]{1,0:T(8,128)(2,1)S(1)}, bf16[64,288]{1,0:T(8,128)(2,1)S(1)}, u32[]{:S(2)}, u32[]{:S(2)}) collective-permute-start(bf16[64,288]{1,0:T(8,128)(2,1)S(1)} %get-tuple-element.251), channel_id=1, source_target_pairs={{0,1},{1,2},{2,3},{3,4},{4,5},{5,6},{6,7},{7,0},{8,9},{9,10},{10,1... | collective-permute-start | bytes 110600 | tf_op jit(solution)/shard_map/while/body/eval_jaxpr/ppermute | solution.py:75
  102.5 4.2 %collective-permute-start.1 = (s32[2,64]{1,0:T(2,128)S(1)}, s32[2,64]{1,0:T(2,128)S(1)}, u32[]{:S(2)}, u32[]{:S(2)}) collective-permute-start(s32[2,64]{1,0:T(2,128)S(1)} %get-tuple-element.252), channel_id=1, source_target_pairs={{0,1},{1,2},{2,3},{3,4},{4,5},{5,6},{6,7},{7,0},{8,9},{9,10},{10,1... | collective-permute-start | bytes 1544 | tf_op jit(solution)/shard_map/while/body/eval_jaxpr/ppermute | solution.py:76
  102.6 5.0 %collective-permute-start = (bf16[64,288]{1,0:T(8,128)(2,1)S(1)}, bf16[64,288]{1,0:T(8,128)(2,1)S(1)}, u32[]{:S(2)}, u32[]{:S(2)}) collective-permute-start(bf16[64,288]{1,0:T(8,128)(2,1)S(1)} %get-tuple-element.251), channel_id=1, source_target_pairs={{0,1},{1,2},{2,3},{3,4},{4,5},{5,6},{6,7},{7,0},{8,9},{9,10},{10,1... | collective-permute-start | bytes 110600 | tf_op jit(solution)/shard_map/while/body/eval_jaxpr/ppermute | solution.py:75
  117.2 4.2 %collective-permute-start.1 = (s32[2,64]{1,0:T(2,128)S(1)}, s32[2,64]{1,0:T(2,128)S(1)}, u32[]{:S(2)}, u32[]{:S(2)}) collective-permute-start(s32[2,64]{1,0:T(2,128)S(1)} %get-tuple-element.252), channel_id=1, source_target_pairs={{0,1},{1,2},{2,3},{3,4},{4,5},{5,6},{6,7},{7,0},{8,9},{9,10},{10,1... | collective-permute-start | bytes 1544 | tf_op jit(solution)/shard_map/while/body/eval_jaxpr/ppermute | solution.py:76
  117.2 5.0 %collective-permute-start = (bf16[64,288]{1,0:T(8,128)(2,1)S(1)}, bf16[64,288]{1,0:T(8,128)(2,1)S(1)}, u32[]{:S(2)}, u32[]{:S(2)}) collective-permute-start(bf16[64,288]{1,0:T(8,128)(2,1)S(1)} %get-tuple-element.251), channel_id=1, source_target_pairs={{0,1},{1,2},{2,3},{3,4},{4,5},{5,6},{6,7},{7,0},{8,9},{9,10},{10,1... | collective-permute-start | bytes 110600 | tf_op jit(solution)/shard_map/while/body/eval_jaxpr/ppermute | solution.py:75
where the time goes:
time: 142 us; the launch traced here: 141 us
  matrix products  88.5 us (62%)
  waiting for transfers between devices  26.7 us (19%)
  other arithmetic  14.2 us (10%)
  local copies, waits for them, and re-layouts  7.74 us (5%)
  starting transfers between devices  3.29 us (2%)
    dot_general x8, matrix products, attend_block(): jnp.einsum('qhk,khd->qhd', weights.astype(jnp.bfloat16), v_blk, preferred...  29.6 us
    dot_general x8, matrix products, attend_block(): jnp.einsum('qhd,khd->qhk', q_nope, k_nope, preferred_element_type=jnp.flo...  29 us
    ppermute x7, waiting for transfers between devices, hop_step(): ids_blk = lax.ppermute(ids_blk, 'ctx', shift_pairs)  26.6 us
    dot_general x8, matrix products, attend_block(): jnp.einsum('qhr,kr->qhk', q_rope, lat_blk[:, kv_rank:], preferred_element...  14.8 us
    dot_general x1, matrix products, per_device(): jnp.dot(attn_out, w_out, preferred_element_type=jnp.float32)  7.87 us
    and x8, other arithmetic, attend_block(): (ids_blk[0][None, :] <= pos_rows[:, None]) & (ids_blk[1][None, :] == seg_...  5.96 us
    unnamed x20, local copies, waits for them, and re-layouts  4.94 us
    dot_general x1, matrix products, per_device(): jnp.dot(x_rows, w_dq, preferred_element_type=jnp.float32)  3.27 us
  transfers between devices with their start and end apart: 14, of which 7 were waited for; matrix products, arithmetic and copies ran while one was open for 4% of the time, Pallas kernels for 0%

commit v1 on v0

v1 whole, which is shorter than its diff:
```python
import functools
import math

import jax
import jax.numpy as jnp
import numpy as np
from jax import lax
from jax.experimental import pallas as pl
from jax.experimental.pallas import tpu as pltpu
from jax.sharding import PartitionSpec as P

NORM_EPS = 1e-6
MASKED = -1e30
LANES = 128
PACK_ROWS = 16
MESH = pl.DeviceIdType.MESH
NT = (((1,), (1,)), ((), ()))
TT = (((0,), (1,)), ((), ()))


def mm(a, b, dims=(((1,), (0,)), ((), ()))):
    return lax.dot_general(a, b, dims, preferred_element_type=jnp.float32)


def rms_norm(vals, gain):
    mean_sq = jnp.mean(vals * vals, axis=-1, keepdims=True)
    return (vals * lax.rsqrt(mean_sq + NORM_EPS) * gain).astype(jnp.bfloat16)


def iota(shape, dim):
    return lax.broadcasted_iota(jnp.int32, shape, dim)


def layer_kernel(n, x_h, pos_h, wdq_h, wuq_h, wqr_h, wdkv_h, wkr_h, wuk_h, wuv_h, wout_h, gq_h, gkv_h, y_h,
                 x_v, pos_v, wdq_v, wuq_v, wqr_v, wdkv_v, wkr_v, wuk_v, wuv_v, wout_v, gq_v, gkv_v,
                 lat, cq_v, qcat, kcat, kr_v, vt, bias_v, o_v, y_v, in_sem, y_sem, send_sem, recv_sem):
    rows, width = x_v.shape
    kv_rank = wdkv_v.shape[1]
    rope = wkr_v.shape[1]
    half_rope = rope // 2
    pairs = kcat.shape[0]
    nope = LANES // 2
    keys = n * rows
    half = rows // 2
    out_chunk = width // y_sem.shape[0]

    me = lax.axis_index("ctx")
    partner = me + 1 - 2 * lax.rem(me, 2)
    others = [lax.rem(me + 2 * k, n) for k in range(1, n // 2)]

    copies = []

    def fetch(src, dst):
        cp = pltpu.make_async_copy(src, dst, in_sem.at[len(copies)])
        cp.start()
        copies.append(cp)
        return cp

    get_pos = fetch(pos_h, pos_v)
    get_x = fetch(x_h, x_v)
    get_wkr = fetch(wkr_h, wkr_v)
    get_wdkv = fetch(wdkv_h, wdkv_v)
    get_gkv = fetch(gkv_h, gkv_v)
    get_gq = fetch(gq_h, gq_v)
    get_wdq = fetch(wdq_h, wdq_v)
    get_wuq = fetch(wuq_h, wuq_v)
    get_wqr = fetch(wqr_h, wqr_v)
    get_wuk = fetch(wuk_h, wuk_v)
    get_wuv = fetch(wuv_h, wuv_v)
    get_wout = [fetch(wout_h.at[:, pl.ds(c * out_chunk, out_chunk)], wout_v.at[:, pl.ds(c * out_chunk, out_chunk)])
                for c in range(y_sem.shape[0])]

    barrier = pltpu.get_barrier_semaphore()
    for peer in [partner] + others:
        pl.semaphore_signal(barrier, inc=1, device_id={"ctx": peer}, device_id_type=MESH)

    get_pos.wait()
    pos_row = pos_v[...].astype(jnp.float32)
    diag = iota((rows, rows), 0) == iota((rows, rows), 1)
    pos_col = jnp.sum(jnp.where(diag, jnp.broadcast_to(pos_row, (rows, rows)), 0.0), axis=1, keepdims=True)
    lane = iota((rows, LANES), 1)
    freq_id = lax.rem(lane, half_rope)
    inv_freq = jnp.zeros((rows, LANES), jnp.float32)
    for f in range(half_rope):
        inv_freq = jnp.where(freq_id == f, float(np.float32(10000.0 ** (-2.0 * f / rope))), inv_freq)
    angles = pos_col * inv_freq
    first = lax.rem(lane, rope) < half_rope
    cos_tab = jnp.cos(angles)
    sin_tab = jnp.sin(angles)
    sin_tab = jnp.where(first, -sin_tab, sin_tab)

    def rope_lanes(a):
        other = jnp.where(first, pltpu.roll(a, LANES - half_rope, 1), pltpu.roll(a, half_rope, 1))
        return (a * cos_tab + other * sin_tab).astype(jnp.bfloat16)

    q_row = iota((rows, LANES), 0)
    q_lane = lax.rem(lane, rows)
    pos_lane = jnp.sum(jnp.where(q_row == q_lane, jnp.broadcast_to(pos_col, (rows, LANES)), 0.0), axis=0, keepdims=True)
    q_lane = q_lane[:1]
    q_seq = jnp.where(q_lane < half, half * me + q_lane, half * (2 * n - 2 - me) + q_lane)
    q_first = q_seq - pos_lane.astype(jnp.int32)
    k_row = iota((keys, LANES), 0)
    k_dev = k_row // rows
    k_in = lax.rem(k_row, rows)
    k_seq = jnp.where(k_in < half, half * k_dev + k_in, half * (2 * n - 2 - k_dev) + k_in)
    bias_v[...] = jnp.where((k_seq >= q_first) & (k_seq <= q_seq), 0.0, MASKED)

    get_x.wait()
    get_wkr.wait()
    kr = mm(x_v[...], wkr_v[...])
    get_wdkv.wait()
    kv = mm(x_v[...], wdkv_v[...])
    get_gkv.wait()
    lat[me, :rows, :] = rms_norm(kv, gkv_v[...].astype(jnp.float32))
    kr = rope_lanes(jnp.concatenate([kr] * (LANES // rope), axis=1))
    packed = jnp.zeros((PACK_ROWS, LANES), jnp.bfloat16)
    slot = iota((PACK_ROWS, LANES), 1) // rope
    for s in range(rows // PACK_ROWS):
        packed = jnp.where(slot == s, kr[s * PACK_ROWS:(s + 1) * PACK_ROWS], packed)
    lat[me, rows:, :LANES] = packed
    lat[me, rows:, LANES:] = jnp.zeros((PACK_ROWS, kv_rank - LANES), jnp.bfloat16)

    pl.semaphore_wait(barrier, n // 2)

    def send(block, peer, index):
        cp = pltpu.make_async_remote_copy(src_ref=lat.at[block], dst_ref=lat.at[block], send_sem=send_sem.at[index],
                                          recv_sem=recv_sem.at[block], device_id={"ctx": peer}, device_id_type=MESH)
        cp.start()
        return cp

    sends = [send(me, peer, k) for k, peer in enumerate(others)]
    sends.append(send(me, partner, len(sends)))

    get_gq.wait()
    get_wdq.wait()
    cq_v[...] = rms_norm(mm(x_v[...], wdq_v[...]), gq_v[...].astype(jnp.float32))
    get_wuq.wait()
    low = lane < nope
    zero = jnp.zeros((rows, LANES), jnp.bfloat16)
    for c in range(pairs // 4):
        q = mm(cq_v[...], wuq_v[:, c * 4 * LANES:(c + 1) * 4 * LANES]).astype(jnp.bfloat16)
        for i in range(4):
            t = q[:, i * LANES:(i + 1) * LANES]
            qcat[c * 4 + i, :rows, :LANES] = jnp.where(low, t, zero)
            qcat[c * 4 + i, rows:, :LANES] = jnp.where(low, zero, t)
    get_wqr.wait()
    per = LANES // rope
    for c in range(pairs * 2 // per // 2):
        q = mm(cq_v[...], wqr_v[:, c * 2 * LANES:(c + 1) * 2 * LANES])
        for i in range(2):
            t = rope_lanes(q[:, i * LANES:(i + 1) * LANES])
            for s in range(per):
                head = (c * 2 + i) * per + s
                at = head % 2 * rows
                qcat[head // 2, at:at + rows, LANES:] = jnp.where(lane // rope == s, t, zero)

    def arrived(block):
        pltpu.make_async_remote_copy(src_ref=lat.at[block], dst_ref=lat.at[block], send_sem=send_sem.at[0],
                                     recv_sem=recv_sem.at[block], device_id={"ctx": partner}, device_id_type=MESH).wait_recv()

    for block in others:
        arrived(block)
        sends.append(send(block, partner, len(sends)))
    arrived(partner)
    for k in range(1, n // 2):
        arrived(lax.rem(partner + 2 * k, n))

    c_all = lat[:, :rows, :].reshape(keys, kv_rank)
    packs = lat[:, rows:, :LANES]
    pslot = iota((n, PACK_ROWS, LANES), 2) // rope
    spread = jnp.stack([jnp.where(pslot == s, packs, jnp.zeros_like(packs)) for s in range(rows // PACK_ROWS)], axis=1)
    same = lax.rem(iota((LANES, LANES), 0), rope) == lax.rem(iota((LANES, LANES), 1), rope)
    kr_v[...] = mm(spread.reshape(keys, LANES), jnp.where(same, 1.0, 0.0).astype(jnp.bfloat16)).astype(jnp.bfloat16)
    get_wuk.wait()
    for c in range(pairs // 2):
        k = mm(c_all, wuk_v[:, c * 2 * LANES:(c + 1) * 2 * LANES]).astype(jnp.bfloat16)
        kcat[2 * c] = k[:, :LANES]
        kcat[2 * c + 1] = k[:, LANES:]
    get_wuv.wait()
    for c in range(pairs // 2):
        cols = slice(c * 2 * LANES, (c + 1) * 2 * LANES)
        vt[cols, :] = mm(wuv_v[:, cols], c_all, TT).astype(jnp.bfloat16)

    factor = (nope + rope) ** -0.5 * math.log2(math.e)

    def attend(p, carry):
        k = jnp.concatenate([kcat[p], kr_v[...]], axis=1)
        t = mm(k, qcat[p], NT) * factor + bias_v[...]
        m = jnp.max(t, axis=0, keepdims=True)
        e = jnp.exp2(t - m)
        total = jnp.sum(e, axis=0, keepdims=True)
        cols = pl.ds(pl.multiple_of(p * LANES, LANES), LANES)
        o = (mm(vt[cols, :], e.astype(jnp.bfloat16)) * (1.0 / total)).T
        o_v[:, cols] = jnp.where(low, o[:rows], o[rows:]).astype(jnp.bfloat16)
        return carry

    lax.fori_loop(0, pairs, attend, 0, unroll=2)

    puts = []
    for c, get in enumerate(get_wout):
        cols = slice(c * out_chunk, (c + 1) * out_chunk)
        get.wait()
        y_v[:, cols] = mm(o_v[...], wout_v[:, cols]).astype(jnp.bfloat16)
        put = pltpu.make_async_copy(y_v.at[:, cols], y_h.at[:, cols], y_sem.at[c])
        put.start()
        puts.append(put)
    for cp in sends:
        cp.wait_send()
    for put in puts:
        put.wait()


def solution(mesh):
    n = mesh.shape["ctx"]
    row_spec = P(("dp", "ctx"), None)
    id_spec = P(("dp", "ctx"))

    def per_device(x, pos, seg, w_dq, w_uq, w_qr, w_dkv, w_kr, w_uk, w_uv, w_out, gain_q, gain_kv):
        rows, width = x.shape
        pairs = w_uq.shape[1] // LANES
        keys = n * rows
        kv_rank = w_dkv.shape[1]
        bf, f32 = jnp.bfloat16, jnp.float32
        args = (x, pos.reshape(1, rows), w_dq, w_uq, w_qr, w_dkv, w_kr, w_uk, w_uv, w_out,
                gain_q.reshape(1, -1), gain_kv.reshape(1, -1))
        out_chunks = 5
        scratch = [pltpu.VMEM(a.shape, a.dtype) for a in args]
        scratch += [
            pltpu.VMEM((n, rows + PACK_ROWS, kv_rank), bf),
            pltpu.VMEM((rows, w_dq.shape[1]), bf),
            pltpu.VMEM((pairs, 2 * rows, 2 * LANES), bf),
            pltpu.VMEM((pairs, keys, LANES), bf),
            pltpu.VMEM((keys, LANES), bf),
            pltpu.VMEM((w_uv.shape[1], keys), bf),
            pltpu.VMEM((keys, LANES), f32),
            pltpu.VMEM((rows, w_uv.shape[1]), bf),
            pltpu.VMEM((rows, width), bf),
            pltpu.SemaphoreType.DMA((len(args) - 1 + out_chunks,)),
            pltpu.SemaphoreType.DMA((out_chunks,)),
            pltpu.SemaphoreType.DMA((n - 1,)),
            pltpu.SemaphoreType.DMA((n,)),
        ]
        return pl.pallas_call(
            functools.partial(layer_kernel, n),
            out_shape=jax.ShapeDtypeStruct(x.shape, bf),
            in_specs=[pl.BlockSpec(memory_space=pl.ANY)] * len(args),
            out_specs=pl.BlockSpec(memory_space=pl.ANY),
            scratch_shapes=scratch,
            compiler_params=pltpu.CompilerParams(collective_id=0, has_side_effects=True, vmem_limit_bytes=60 << 20),
        )(*args)

    return jax.shard_map(per_device, mesh=mesh, in_specs=(row_spec, id_spec, id_spec) + (P(),) * 10, out_specs=row_spec, check_vma=False)
```

time: 142 us -> 32 us (0.23)
  the two profiles are of different devices: /device:TPU:112 before, /device:TPU:113 now
where the time goes in v1:
time: 32 us; the launch traced here: 31.9 us
  Pallas kernels  25.7 us (80%)
  local copies, waits for them, and re-layouts  6.2 us (19%)
    pallas_call x1, Pallas kernels, per_device(): pl.pallas_call(functools.partial(layer_kernel, n), out_shape=jax.ShapeDty...  25.7 us
    unnamed x2, local copies, waits for them, and re-layouts  3.71 us
    reshape x1, local copies, waits for them, and re-layouts, per_device(): gain_q.reshape(1, -1)  1.26 us
    reshape x1, local copies, waits for them, and re-layouts, per_device(): gain_kv.reshape(1, -1)  1.23 us

profile of v1, /device:TPU:113, one launch (start us, length us, event | category | flops | bytes accessed | tf_op | source)
XLA Modules:
  0.0 31.9 jit_solution(11783139598583768958)
XLA Ops:
  0.0 1.2 %reshape.11.gkv_h = bf16[1,256]{1,0:T(2,128)(2,1)} reshape(bf16[256]{0:T(256)(128)(2,1)} %param.24) | data formatting | bytes 1024 | tf_op jit(solution)/shard_map/reshape | solution.py:225
  1.2 1.3 %reshape.10.gq_h = bf16[1,768]{1,0:T(2,128)(2,1)} reshape(bf16[768]{0:T(1024)(128)(2,1)} %param.23) | data formatting | bytes 3072 | tf_op jit(solution)/shard_map/reshape | solution.py:225
  2.5 2.0 %copy.13.wkr_h = bf16[2560,32]{1,0:T(8,128)(2,1)} copy(bf16[2560,32]{0,1:T(8,128)(2,1)} %param.19) | data formatting | bytes 327680 | tf_op args[7]
  4.5 25.7 %shard_map.118 = bf16[64,2560]{1,0:T(8,128)(2,1)} custom-call(bf16[64,2560]{1,0:T(8,128)(2,1)} %x_h.1, s32[1,64]{1,0:T(1,128)} %bitcast.1, bf16[2560,768]{1,0:T(8,128)(2,1)} %wdq_h.1, bf16[768,2560]{1,0:T(8,128)(2,1)} %wuq_h.1, bf16[768,1280]{1,0:T(8,128)(2,1)} %wqr_h.1, bf16[2560,256]{1,0:T(8,128)(2,1)} %wdkv_h.1, bf16[2560,32]{1,0:T(8,128)(2,1)} %copy.13.wkr_h, ...), custom_call_target="tpu_custom_call" | custom-call | tf_op jit(solution)/shard_map/pallas_call | solution.py:243
  30.1 1.7 %copy.15 = bf16[64,2560]{1,0:T(8,128)(2,1)} copy(bf16[64,2560]{1,0:T(8,128)(2,1)} %shard_map.118) | data formatting | bytes 655360

commit v2 on v1

--- a/solution.py
+++ b/solution.py
@@ -13,6 +13,8 @@
 MASKED = -1e30
 LANES = 128
 PACK_ROWS = 16
+GROUP = 2
+OUT_CHUNKS = 5
 MESH = pl.DeviceIdType.MESH
 NT = (((1,), (1,)), ((), ()))
 TT = (((0,), (1,)), ((), ()))
@@ -31,18 +33,18 @@
     return lax.broadcasted_iota(jnp.int32, shape, dim)
 
 
-def layer_kernel(n, x_h, pos_h, wdq_h, wuq_h, wqr_h, wdkv_h, wkr_h, wuk_h, wuv_h, wout_h, gq_h, gkv_h, y_h,
+def layer_kernel(n, x_h, pos_h, wdq_h, wuq_h, wqr_h, wdkv_h, wkr_h, wuk_h, wuv_h, wout_h, gq_h, gkv_h, y_v,
                  x_v, pos_v, wdq_v, wuq_v, wqr_v, wdkv_v, wkr_v, wuk_v, wuv_v, wout_v, gq_v, gkv_v,
-                 lat, cq_v, qcat, kcat, kr_v, vt, bias_v, o_v, y_v, in_sem, y_sem, send_sem, recv_sem):
+                 lat, cq_v, qcat, kcat, kr_v, vt, bias_v, o_v, s_v, m_v, p_v, l_v, in_sem, send_sem, recv_sem):
     rows, width = x_v.shape
     kv_rank = wdkv_v.shape[1]
-    rope = wkr_v.shape[1]
+    rope = wkr_v.shape[0]
     half_rope = rope // 2
     pairs = kcat.shape[0]
     nope = LANES // 2
     keys = n * rows
     half = rows // 2
-    out_chunk = width // y_sem.shape[0]
+    out_chunk = width // OUT_CHUNKS
 
     me = lax.axis_index("ctx")
     partner = me + 1 - 2 * lax.rem(me, 2)
@@ -68,7 +70,7 @@
     get_wuk = fetch(wuk_h, wuk_v)
     get_wuv = fetch(wuv_h, wuv_v)
     get_wout = [fetch(wout_h.at[:, pl.ds(c * out_chunk, out_chunk)], wout_v.at[:, pl.ds(c * out_chunk, out_chunk)])
-                for c in range(y_sem.shape[0])]
+                for c in range(OUT_CHUNKS)]
 
     barrier = pltpu.get_barrier_semaphore()
     for peer in [partner] + others:
@@ -107,11 +109,11 @@
 
     get_x.wait()
     get_wkr.wait()
-    kr = mm(x_v[...], wkr_v[...])
+    kr = mm(x_v[...], wkr_v[...], NT)
     get_wdkv.wait()
     kv = mm(x_v[...], wdkv_v[...])
     get_gkv.wait()
-    lat[me, :rows, :] = rms_norm(kv, gkv_v[...].astype(jnp.float32))
+    lat[me, :rows, :] = rms_norm(kv, gkv_v[...].astype(jnp.float32).reshape(1, -1))
     kr = rope_lanes(jnp.concatenate([kr] * (LANES // rope), axis=1))
     packed = jnp.zeros((PACK_ROWS, LANES), jnp.bfloat16)
     slot = iota((PACK_ROWS, LANES), 1) // rope
@@ -133,7 +135,7 @@
 
     get_gq.wait()
     get_wdq.wait()
-    cq_v[...] = rms_norm(mm(x_v[...], wdq_v[...]), gq_v[...].astype(jnp.float32))
+    cq_v[...] = rms_norm(mm(x_v[...], wdq_v[...]), gq_v[...].astype(jnp.float32).reshape(1, -1))
     get_wuq.wait()
     low = lane < nope
     zero = jnp.zeros((rows, LANES), jnp.bfloat16)
@@ -182,32 +184,42 @@
         vt[cols, :] = mm(wuv_v[:, cols], c_all, TT).astype(jnp.bfloat16)
 
     factor = (nope + rope) ** -0.5 * math.log2(math.e)
-
-    def attend(p, carry):
-        k = jnp.concatenate([kcat[p], kr_v[...]], axis=1)
-        t = mm(k, qcat[p], NT) * factor + bias_v[...]
-        m = jnp.max(t, axis=0, keepdims=True)
-        e = jnp.exp2(t - m)
-        total = jnp.sum(e, axis=0, keepdims=True)
-        cols = pl.ds(pl.multiple_of(p * LANES, LANES), LANES)
-        o = (mm(vt[cols, :], e.astype(jnp.bfloat16)) * (1.0 / total)).T
-        o_v[:, cols] = jnp.where(low, o[:rows], o[rows:]).astype(jnp.bfloat16)
-        return carry
-
-    lax.fori_loop(0, pairs, attend, 0, unroll=2)
-
-    puts = []
-    for c, get in enumerate(get_wout):
+    steps = pairs // GROUP
+
+    def scores(g):
+        for i in range(GROUP):
+            k = jnp.concatenate([kcat[g * GROUP + i], kr_v[...]], axis=1)
+            t = mm(k, qcat[g * GROUP + i], NT) * factor + bias_v[...]
+            s_v[g % 2, i] = t
+            m_v[g % 2, i] = jnp.max(t, axis=0, keepdims=True)
+
+    def weights(g):
+        for i in range(GROUP):
+            e = jnp.exp2(s_v[g % 2, i] - m_v[g % 2, i])
+            p_v[g % 2, i] = e.astype(jnp.bfloat16)
+            l_v[g % 2, i] = 1.0 / jnp.sum(e, axis=0, keepdims=True)
+
+    def values(g):
+        for i in range(GROUP):
+            cols = slice((g * GROUP + i) * LANES, (g * GROUP + i + 1) * LANES)
+            o = (mm(vt[cols, :], p_v[g % 2, i]) * l_v[g % 2, i]).T
+            o_v[:, cols] = jnp.where(low, o[:rows], o[rows:]).astype(jnp.bfloat16)
+
+    for g in range(steps + 2):
+        if g >= 2:
+            values(g - 2)
+        if 1 <= g <= steps:
+            weights(g - 1)
+        if g < steps:
+            scores(g)
+
+    for get in get_wout:
+        get.wait()
+    for c in range(len(get_wout)):
         cols = slice(c * out_chunk, (c + 1) * out_chunk)
-        get.wait()
         y_v[:, cols] = mm(o_v[...], wout_v[:, cols]).astype(jnp.bfloat16)
-        put = pltpu.make_async_copy(y_v.at[:, cols], y_h.at[:, cols], y_sem.at[c])
-        put.start()
-        puts.append(put)
     for cp in sends:
         cp.wait_send()
-    for put in puts:
-        put.wait()
 
 
 def solution(mesh):
@@ -221,9 +233,8 @@
         keys = n * rows
         kv_rank = w_dkv.shape[1]
         bf, f32 = jnp.bfloat16, jnp.float32
-        args = (x, pos.reshape(1, rows), w_dq, w_uq, w_qr, w_dkv, w_kr, w_uk, w_uv, w_out,
-                gain_q.reshape(1, -1), gain_kv.reshape(1, -1))
-        out_chunks = 5
+        args = (x, pos.reshape(1, rows), w_dq, w_uq, w_qr, w_dkv, w_kr.T, w_uk, w_uv, w_out,
+                gain_q, gain_kv)
         scratch = [pltpu.VMEM(a.shape, a.dtype) for a in args]
         scratch += [
             pltpu.VMEM((n, rows + PACK_ROWS, kv_rank), bf),
@@ -234,19 +245,21 @@
             pltpu.VMEM((w_uv.shape[1], keys), bf),
             pltpu.VMEM((keys, LANES), f32),
             pltpu.VMEM((rows, w_uv.shape[1]), bf),
-            pltpu.VMEM((rows, width), bf),
-            pltpu.SemaphoreType.DMA((len(args) - 1 + out_chunks,)),
-            pltpu.SemaphoreType.DMA((out_chunks,)),
+            pltpu.VMEM((2, GROUP, keys, LANES), f32),
+            pltpu.VMEM((2, GROUP, 1, LANES), f32),
+            pltpu.VMEM((2, GROUP, keys, LANES), bf),
+            pltpu.VMEM((2, GROUP, 1, LANES), f32),
+            pltpu.SemaphoreType.DMA((len(args) - 1 + OUT_CHUNKS,)),
             pltpu.SemaphoreType.DMA((n - 1,)),
             pltpu.SemaphoreType.DMA((n,)),
         ]
         return pl.pallas_call(
             functools.partial(layer_kernel, n),
             out_shape=jax.ShapeDtypeStruct(x.shape, bf),
-            in_specs=[pl.BlockSpec(memory_space=pl.ANY)] * len(args),
-            out_specs=pl.BlockSpec(memory_space=pl.ANY),
+            in_specs=[pl.BlockSpec(memory_space=pltpu.HBM)] * len(args),
+            out_specs=pl.BlockSpec(memory_space=pltpu.VMEM),
             scratch_shapes=scratch,
-            compiler_params=pltpu.CompilerParams(collective_id=0, has_side_effects=True, vmem_limit_bytes=60 << 20),
+            compiler_params=pltpu.CompilerParams(collective_id=0, has_side_effects=True, vmem_limit_bytes=62000000),
         )(*args)
 
     return jax.shard_map(per_device, mesh=mesh, in_specs=(row_spec, id_spec, id_spec) + (P(),) * 10, out_specs=row_spec, check_vma=False)

time: 32 us -> 19.9 us (0.62)
  Pallas kernels: 25.7 us -> 18.1 us
  local copies, waits for them, and re-layouts: 6.2 us -> 1.72 us
    pallas_call x1, Pallas kernels: 25.7 us -> 18.1 us  [per_device(): pl.pallas_call(functools.partial(layer_kernel, n), out_shape=jax.ShapeDty...]
    reshape x2 -> x0, local copies, waits for them, and re-layouts: 2.49 us -> none  [the longest x1 1.26 us: per_device(): gain_q.reshape(1, -1)]
    unnamed x2 -> x1, local copies, waits for them, and re-layouts: 3.71 us -> 1.72 us
where the time goes in v2:
time: 19.9 us; the launch traced here: 19.8 us
  Pallas kernels  18.1 us (91%)
  local copies, waits for them, and re-layouts  1.72 us (9%)
    pallas_call x1, Pallas kernels, per_device(): pl.pallas_call(functools.partial(layer_kernel, n), out_shape=jax.ShapeDty...  18.1 us
    unnamed x1, local copies, waits for them, and re-layouts  1.72 us

profile of v2, /device:TPU:113, one launch (start us, length us, event | category | flops | bytes accessed | tf_op | source)
XLA Modules:
  0.0 19.8 jit_solution(10686002541781471329)
XLA Ops:
  0.0 18.1 %shard_map.118 = bf16[64,2560]{1,0:T(8,128)(2,1)} custom-call(bf16[64,2560]{1,0:T(8,128)(2,1)} %x_h.1, s32[1,64]{1,0:T(1,128)} %bitcast.3, bf16[2560,768]{1,0:T(8,128)(2,1)} %wdq_h.1, bf16[768,2560]{1,0:T(8,128)(2,1)} %wuq_h.1, bf16[768,1280]{1,0:T(8,128)(2,1)} %wqr_h.1, bf16[2560,256]{1,0:T(8,128)(2,1)} %wdkv_h.1, bf16[32,2560]{1,0:T(8,128)(2,1)} %bitcast.2, ...), custom_call_target="tpu_custom_call" | custom-call | tf_op jit(solution)/shard_map/pallas_call | solution.py:256
  18.1 1.7 %copy.14 = bf16[64,2560]{1,0:T(8,128)(2,1)} copy(bf16[64,2560]{1,0:T(8,128)(2,1)} %shard_map.118) | data formatting | bytes 655360

commit v3 on v2

--- a/solution.py
+++ b/solution.py
@@ -50,13 +50,15 @@
     partner = me + 1 - 2 * lax.rem(me, 2)
     others = [lax.rem(me + 2 * k, n) for k in range(1, n // 2)]
 
-    copies = []
+    fetches = []
 
     def fetch(src, dst):
-        cp = pltpu.make_async_copy(src, dst, in_sem.at[len(copies)])
-        cp.start()
-        copies.append(cp)
-        return cp
+        fetches.append(pltpu.make_async_copy(src, dst, in_sem.at[len(fetches)]))
+        return fetches[-1]
+
+    def start(*copies):
+        for cp in copies:
+            cp.start()
 
     get_pos = fetch(pos_h, pos_v)
     get_x = fetch(x_h, x_v)
@@ -71,6 +73,7 @@
     get_wuv = fetch(wuv_h, wuv_v)
     get_wout = [fetch(wout_h.at[:, pl.ds(c * out_chunk, out_chunk)], wout_v.at[:, pl.ds(c * out_chunk, out_chunk)])
                 for c in range(OUT_CHUNKS)]
+    start(get_pos, get_x, get_wkr, get_wdkv, get_gkv, get_gq, get_wdq)
 
     barrier = pltpu.get_barrier_semaphore()
     for peer in [partner] + others:
@@ -111,6 +114,7 @@
     get_wkr.wait()
     kr = mm(x_v[...], wkr_v[...], NT)
     get_wdkv.wait()
+    start(get_wuq, get_wqr, get_wuk, get_wuv)
     kv = mm(x_v[...], wdkv_v[...])
     get_gkv.wait()
     lat[me, :rows, :] = rms_norm(kv, gkv_v[...].astype(jnp.float32).reshape(1, -1))
@@ -135,6 +139,7 @@
 
     get_gq.wait()
     get_wdq.wait()
+    start(*get_wout)
     cq_v[...] = rms_norm(mm(x_v[...], wdq_v[...]), gq_v[...].astype(jnp.float32).reshape(1, -1))
     get_wuq.wait()
     low = lane < nope

time: 19.9 us -> 19.9 us (level)
  no operation moved by 1% of the time
where the time goes in v3:
time: 19.9 us; the launch traced here: 19.8 us
  Pallas kernels  18.1 us (91%)
  local copies, waits for them, and re-layouts  1.72 us (9%)
    pallas_call x1, Pallas kernels, per_device(): pl.pallas_call(functools.partial(layer_kernel, n), out_shape=jax.ShapeDty...  18.1 us
    unnamed x1, local copies, waits for them, and re-layouts  1.72 us

profile of v3, /device:TPU:113, one launch (start us, length us, event | category | flops | bytes accessed | tf_op | source)
XLA Modules:
  0.0 19.8 jit_solution(7623540926426546519)
XLA Ops:
  0.0 18.1 %shard_map.118 = bf16[64,2560]{1,0:T(8,128)(2,1)} custom-call(bf16[64,2560]{1,0:T(8,128)(2,1)} %x_h.1, s32[1,64]{1,0:T(1,128)} %bitcast.3, bf16[2560,768]{1,0:T(8,128)(2,1)} %wdq_h.1, bf16[768,2560]{1,0:T(8,128)(2,1)} %wuq_h.1, bf16[768,1280]{1,0:T(8,128)(2,1)} %wqr_h.1, bf16[2560,256]{1,0:T(8,128)(2,1)} %wdkv_h.1, bf16[32,2560]{1,0:T(8,128)(2,1)} %bitcast.2, ...), custom_call_target="tpu_custom_call" | custom-call | tf_op jit(solution)/shard_map/pallas_call | solution.py:261
  18.1 1.7 %copy.14 = bf16[64,2560]{1,0:T(8,128)(2,1)} copy(bf16[64,2560]{1,0:T(8,128)(2,1)} %shard_map.118) | data formatting | bytes 655360

commit v4 on v3

--- a/solution.py
+++ b/solution.py
@@ -47,8 +47,7 @@
     out_chunk = width // OUT_CHUNKS
 
     me = lax.axis_index("ctx")
-    partner = me + 1 - 2 * lax.rem(me, 2)
-    others = [lax.rem(me + 2 * k, n) for k in range(1, n // 2)]
+    peers = [lax.rem(me + k, n) for k in range(1, n)]
 
     fetches = []
 
@@ -76,7 +75,7 @@
     start(get_pos, get_x, get_wkr, get_wdkv, get_gkv, get_gq, get_wdq)
 
     barrier = pltpu.get_barrier_semaphore()
-    for peer in [partner] + others:
+    for peer in peers:
         pl.semaphore_signal(barrier, inc=1, device_id={"ctx": peer}, device_id_type=MESH)
 
     get_pos.wait()
@@ -126,7 +125,7 @@
     lat[me, rows:, :LANES] = packed
     lat[me, rows:, LANES:] = jnp.zeros((PACK_ROWS, kv_rank - LANES), jnp.bfloat16)
 
-    pl.semaphore_wait(barrier, n // 2)
+    pl.semaphore_wait(barrier, n - 1)
 
     def send(block, peer, index):
         cp = pltpu.make_async_remote_copy(src_ref=lat.at[block], dst_ref=lat.at[block], send_sem=send_sem.at[index],
@@ -134,8 +133,8 @@
         cp.start()
         return cp
 
-    sends = [send(me, peer, k) for k, peer in enumerate(others)]
-    sends.append(send(me, partner, len(sends)))
+    order = sorted(range(n - 1), key=lambda k: -min(k + 1, n - 1 - k))
+    sends = [send(me, peers[k], k) for k in order]
 
     get_gq.wait()
     get_wdq.wait()
@@ -161,16 +160,9 @@
                 at = head % 2 * rows
                 qcat[head // 2, at:at + rows, LANES:] = jnp.where(lane // rope == s, t, zero)
 
-    def arrived(block):
+    for block in peers:
         pltpu.make_async_remote_copy(src_ref=lat.at[block], dst_ref=lat.at[block], send_sem=send_sem.at[0],
-                                     recv_sem=recv_sem.at[block], device_id={"ctx": partner}, device_id_type=MESH).wait_recv()
-
-    for block in others:
-        arrived(block)
-        sends.append(send(block, partner, len(sends)))
-    arrived(partner)
-    for k in range(1, n // 2):
-        arrived(lax.rem(partner + 2 * k, n))
+                                     recv_sem=recv_sem.at[block], device_id={"ctx": block}, device_id_type=MESH).wait_recv()
 
     c_all = lat[:, :rows, :].reshape(keys, kv_rank)
     packs = lat[:, rows:, :LANES]

time: 19.9 us -> 20.1 us (1.010)
  the two profiles are of different devices: /device:TPU:113 before, /device:TPU:112 now
where the time goes in v4:
time: 20.1 us; the launch traced here: 20 us
  Pallas kernels  18.2 us (91%)
  local copies, waits for them, and re-layouts  1.72 us (9%)
    pallas_call x1, Pallas kernels, per_device(): pl.pallas_call(functools.partial(layer_kernel, n), out_shape=jax.ShapeDty...  18.2 us
    unnamed x1, local copies, waits for them, and re-layouts  1.72 us

profile of v4, /device:TPU:112, one launch (start us, length us, event | category | flops | bytes accessed | tf_op | source)
XLA Modules:
  0.0 20.0 jit_solution(10754571205584870326)
XLA Ops:
  0.0 18.2 %shard_map.118 = bf16[64,2560]{1,0:T(8,128)(2,1)} custom-call(bf16[64,2560]{1,0:T(8,128)(2,1)} %x_h.1, s32[1,64]{1,0:T(1,128)} %bitcast.3, bf16[2560,768]{1,0:T(8,128)(2,1)} %wdq_h.1, bf16[768,2560]{1,0:T(8,128)(2,1)} %wuq_h.1, bf16[768,1280]{1,0:T(8,128)(2,1)} %wqr_h.1, bf16[2560,256]{1,0:T(8,128)(2,1)} %wdkv_h.1, bf16[32,2560]{1,0:T(8,128)(2,1)} %bitcast.2, ...), custom_call_target="tpu_custom_call" | custom-call | tf_op jit(solution)/shard_map/pallas_call | solution.py:253
  18.2 1.7 %copy.14 = bf16[64,2560]{1,0:T(8,128)(2,1)} copy(bf16[64,2560]{1,0:T(8,128)(2,1)} %shard_map.118) | data formatting | bytes 655360

commit v5 on v4

--- a/solution.py
+++ b/solution.py
@@ -252,7 +252,7 @@
         ]
         return pl.pallas_call(
             functools.partial(layer_kernel, n),
-            out_shape=jax.ShapeDtypeStruct(x.shape, bf),
+            out_shape=pltpu.VMEM(x.shape, bf),
             in_specs=[pl.BlockSpec(memory_space=pltpu.HBM)] * len(args),
             out_specs=pl.BlockSpec(memory_space=pltpu.VMEM),
             scratch_shapes=scratch,

time: 20.1 us -> 18.3 us (0.910)
  local copies, waits for them, and re-layouts: 1.72 us -> 0.73 us
  Pallas kernels: 18.2 us -> 17.5 us
    unnamed x1, local copies, waits for them, and re-layouts: 1.72 us -> 0.73 us
    pallas_call x1, Pallas kernels: 18.2 us -> 17.5 us  [per_device(): pl.pallas_call(functools.partial(layer_kernel, n), out_shape=pltpu.VMEM(x...]
where the time goes in v5:
time: 18.3 us
  Pallas kernels  17.5 us (96%)
  local copies, waits for them, and re-layouts  0.73 us (4%)
    pallas_call x1, Pallas kernels, per_device(): pl.pallas_call(functools.partial(layer_kernel, n), out_shape=pltpu.VMEM(x...  17.5 us
    unnamed x1, local copies, waits for them, and re-layouts  0.73 us

profile of v5, /device:TPU:112, one launch (start us, length us, event | category | flops | bytes accessed | tf_op | source)
XLA Modules:
  0.0 18.3 jit_solution(13374045886597604803)
XLA Ops:
  0.0 17.5 %shard_map.118 = bf16[64,2560]{1,0:T(8,128)(2,1)S(1)} custom-call(bf16[64,2560]{1,0:T(8,128)(2,1)} %x_h.1, s32[1,64]{1,0:T(1,128)} %bitcast.3, bf16[2560,768]{1,0:T(8,128)(2,1)} %wdq_h.1, bf16[768,2560]{1,0:T(8,128)(2,1)} %wuq_h.1, bf16[768,1280]{1,0:T(8,128)(2,1)} %wqr_h.1, bf16[2560,256]{1,0:T(8,128)(2,1)} %wdkv_h.1, bf16[32,2560]{1,0:T(8,128)(2,1)} %bitcast.2, ...), custom_call_target="tpu_custom_call" | custom-call | tf_op jit(solution)/shard_map/pallas_call | solution.py:253
  17.5 0.7 %copy.14 = bf16[64,2560]{1,0:T(8,128)(2,1)} copy(bf16[64,2560]{1,0:T(8,128)(2,1)S(1)} %shard_map.118) | data formatting | bytes 655360

commit v6 on v5

v6 whole, which is shorter than its diff:
```python
import functools
import math

import jax
import jax.numpy as jnp
import numpy as np
from jax import lax
from jax.experimental import pallas as pl
from jax.experimental.pallas import tpu as pltpu
from jax.sharding import PartitionSpec as P

NORM_EPS = 1e-6
MASKED = -1e30
LANES = 128
PACK_ROWS = 16
GROUP = 2
OUT_CHUNKS = 5
MESH = pl.DeviceIdType.MESH
NT = (((1,), (1,)), ((), ()))


def mm(a, b, dims=(((1,), (0,)), ((), ()))):
    return lax.dot_general(a, b, dims, preferred_element_type=jnp.float32)


def rms_norm(vals, gain):
    mean_sq = jnp.mean(vals * vals, axis=-1, keepdims=True)
    return (vals * lax.rsqrt(mean_sq + NORM_EPS) * gain).astype(jnp.bfloat16)


def iota(shape, dim):
    return lax.broadcasted_iota(jnp.int32, shape, dim)


def layer_kernel(n, x_h, pos_h, wdq_h, wuq_h, wqr_h, wdkv_h, wkr_h, wuk_h, wuv_h, wout_h, gq_h, gkv_h, y_v,
                 x_v, pos_v, wdq_v, wuq_v, wqr_v, wdkv_v, wkr_v, wuk_v, wuv_v, wout_v, gq_v, gkv_v,
                 lat, cq_v, qcat, kt_v, krt_v, v_v, bias_v, o_v, s_v, p_v, l_v, in_sem, send_sem, recv_sem):
    rows, width = x_v.shape
    kv_rank = wdkv_v.shape[1]
    rope = wkr_v.shape[0]
    half_rope = rope // 2
    pairs = kt_v.shape[0]
    nope = LANES // 2
    half = rows // 2
    chips = n // 2
    keys = chips * rows
    short = half + PACK_ROWS
    out_chunk = width // OUT_CHUNKS

    me = lax.axis_index("ctx")
    my_chip = me // 2
    peers = [lax.rem(me + k, n) for k in range(1, n)]

    barrier = pltpu.get_barrier_semaphore()
    for peer in peers:
        pl.semaphore_signal(barrier, inc=1, device_id={"ctx": peer}, device_id_type=MESH)

    fetches = []

    def fetch(src, dst):
        fetches.append(pltpu.make_async_copy(src, dst, in_sem.at[len(fetches)]))
        return fetches[-1]

    def start(*copies):
        for cp in copies:
            cp.start()

    get_pos = fetch(pos_h, pos_v)
    get_x = fetch(x_h, x_v)
    get_wkr = fetch(wkr_h, wkr_v)
    get_wdkv = fetch(wdkv_h, wdkv_v)
    get_gkv = fetch(gkv_h, gkv_v)
    get_gq = fetch(gq_h, gq_v)
    get_wdq = fetch(wdq_h, wdq_v)
    get_wuq = fetch(wuq_h, wuq_v)
    get_wqr = fetch(wqr_h, wqr_v)
    get_wuk = fetch(wuk_h, wuk_v)
    get_wuv = fetch(wuv_h, wuv_v)
    get_wout = [fetch(wout_h.at[:, pl.ds(c * out_chunk, out_chunk)], wout_v.at[:, pl.ds(c * out_chunk, out_chunk)])
                for c in range(OUT_CHUNKS)]
    start(get_pos, get_x, get_wkr, get_wdkv, get_gkv, get_gq, get_wdq)

    get_pos.wait()
    pos_row = pos_v[...].astype(jnp.float32)

    def pos_of(count, index):
        spot = iota((count, rows), 1) == index(iota((count, rows), 0))
        return jnp.sum(jnp.where(spot, jnp.broadcast_to(pos_row, (count, rows)), 0.0), axis=1, keepdims=True)

    lane = iota((rows, LANES), 1)
    freq_id = lax.rem(lane[:1], half_rope)
    inv_freq = jnp.zeros((1, LANES), jnp.float32)
    for f in range(half_rope):
        inv_freq = jnp.where(freq_id == f, float(np.float32(10000.0 ** (-2.0 * f / rope))), inv_freq)
    angles = pos_of(rows, lambda r: r) * inv_freq
    first = lax.rem(lane, rope) < half_rope
    cos_tab = jnp.cos(angles)
    sin_tab = jnp.sin(angles)
    sin_tab = jnp.where(first, -sin_tab, sin_tab)

    def rope_lanes(a):
        other = jnp.where(first, pltpu.roll(a, LANES - half_rope, 1), pltpu.roll(a, half_rope, 1))
        return (a * cos_tab + other * sin_tab).astype(jnp.bfloat16)

    count = 2 * rows
    q_pos = pos_of(count, lambda r: lax.rem(r, half) + jnp.where(r >= rows, half, 0)).astype(jnp.int32)
    q_row = iota((count, 1), 0)
    q_seq = jnp.where(q_row < rows, half * me, half * (2 * n - 1 - me)) + lax.rem(q_row, half)
    q_first = q_seq - q_pos
    col = iota((1, keys), 1)
    slot = col // rows
    swapped = slot + 1 - 2 * lax.rem(slot, 2)
    inner = lax.rem(col, rows)

    def key_seq(slot, late):
        dev = 2 * lax.rem(my_chip + slot, chips) + inner // half
        return half * jnp.where(late, 2 * n - 1 - dev, dev) + lax.rem(inner, half)

    def visible(seq, lo, hi):
        return jnp.where((seq >= lo) & (seq <= hi), 0.0, MASKED)

    bias_v[:count] = visible(key_seq(slot, False), q_first, q_seq)
    bias_v[count:] = visible(key_seq(swapped, True), q_first[rows:], q_seq[rows:])

    for peer in peers:
        @pl.when(peer < me)
        def _():
            lat[peer, short:, :] = jnp.zeros((half, kv_rank), jnp.bfloat16)

    get_x.wait()
    get_wkr.wait()
    kr = mm(x_v[...], wkr_v[...], NT)
    get_wdkv.wait()
    start(get_wuq, get_wqr, get_wuk, get_wuv)
    kv = mm(x_v[...], wdkv_v[...])
    get_gkv.wait()
    c_kv = rms_norm(kv, gkv_v[...].astype(jnp.float32).reshape(1, -1))
    lat[me, :half, :] = c_kv[:half]
    lat[me, short:, :] = c_kv[half:]
    kr = rope_lanes(jnp.concatenate([kr] * (LANES // rope), axis=1))
    packed = jnp.zeros((PACK_ROWS, LANES), jnp.bfloat16)
    part = iota((PACK_ROWS, LANES), 1) // rope
    for s in range(rows // PACK_ROWS):
        packed = jnp.where(part == s, kr[s * PACK_ROWS:(s + 1) * PACK_ROWS], packed)
    lat[me, half:short, :LANES] = packed
    lat[me, half:short, LANES:] = jnp.zeros((PACK_ROWS, kv_rank - LANES), jnp.bfloat16)

    pl.semaphore_wait(barrier, n - 1)

    def push(block, peer, index, count):
        at = lat.at[block, pl.ds(0, count)]
        return pltpu.make_async_remote_copy(src_ref=at, dst_ref=at, send_sem=send_sem.at[index],
                                            recv_sem=recv_sem.at[block], device_id={"ctx": peer}, device_id_type=MESH)

    def send(k):
        @pl.when(peers[k] < me)
        def _():
            push(me, peers[k], k, short + half).start()

        @pl.when(peers[k] > me)
        def _():
            push(me, peers[k], k, short).start()

    def sent(k):
        @pl.when(peers[k] < me)
        def _():
            push(me, peers[k], k, short + half).wait_send()

        @pl.when(peers[k] > me)
        def _():
            push(me, peers[k], k, short).wait_send()

    def arrived(block):
        @pl.when(block > me)
        def _():
            push(block, me, 0, short + half).wait_recv()

        @pl.when(block < me)
        def _():
            push(block, me, 0, short).wait_recv()

    for k in sorted(range(n - 1), key=lambda k: -min(k + 1, n - 1 - k)):
        send(k)

    get_gq.wait()
    get_wdq.wait()
    start(*get_wout)
    cq_v[...] = rms_norm(mm(x_v[...], wdq_v[...]), gq_v[...].astype(jnp.float32).reshape(1, -1))
    low = lane < nope
    zero = jnp.zeros((rows, LANES), jnp.bfloat16)

    def put_query(head, cols, t):
        at = head % 2 * half
        qcat[head // 2, at:at + half, cols] = t[:half]
        qcat[head // 2, rows + at:rows + at + half, cols] = t[half:]

    get_wuq.wait()
    for c in range(pairs // 4):
        q = mm(cq_v[...], wuq_v[:, c * 4 * LANES:(c + 1) * 4 * LANES]).astype(jnp.bfloat16)
        for i in range(4):
            t = q[:, i * LANES:(i + 1) * LANES]
            put_query(2 * (c * 4 + i), slice(0, LANES), jnp.where(low, t, zero))
            put_query(2 * (c * 4 + i) + 1, slice(0, LANES), jnp.where(low, zero, t))
    get_wqr.wait()
    per = LANES // rope
    for c in range(pairs // per):
        q = mm(cq_v[...], wqr_v[:, c * 2 * LANES:(c + 1) * 2 * LANES])
        for i in range(2):
            t = rope_lanes(q[:, i * LANES:(i + 1) * LANES])
            for s in range(per):
                put_query((c * 2 + i) * per + s, slice(LANES, 2 * LANES), jnp.where(lane // rope == s, t, zero))

    same = lax.rem(iota((LANES, LANES), 0), rope) == lax.rem(iota((LANES, LANES), 1), rope)
    same = jnp.where(same, 1.0, 0.0).astype(jnp.bfloat16)

    def up_project(t):
        chip = lax.rem(my_chip + t, chips)
        block = lat[pl.ds(2 * chip, 2)]
        pieces = [block[:, :half].reshape(rows, kv_rank), block[:, short:].reshape(rows, kv_rank)]
        groups = half // PACK_ROWS
        spread = [[jnp.where(part == p * groups + s, block[d, half:short, :LANES], jnp.zeros((PACK_ROWS, LANES), jnp.bfloat16))
                   for d in range(2) for s in range(groups)] for p in range(2)]
        first_piece = t % 2
        order = [first_piece, 1 - first_piece]
        c_chip = jnp.concatenate([pieces[p] for p in order], axis=0)
        krt = mm(same, jnp.concatenate(spread[order[0]] + spread[order[1]], axis=0), NT).astype(jnp.bfloat16)
        spots = [(order[i], (t - t % 2 + i) * rows, i * rows) for i in range(2)]
        for p, at, src in spots:
            krt_v[p, :, at:at + rows] = krt[:, src:src + rows]
        for c in range(pairs // 2):
            cols = slice(c * 2 * LANES, (c + 1) * 2 * LANES)
            k = mm(c_chip, wuk_v[:, cols]).astype(jnp.bfloat16)
            v = mm(c_chip, wuv_v[:, cols]).astype(jnp.bfloat16)
            for p, at, src in spots:
                v_v[p, at:at + rows, cols] = v[src:src + rows]
            for i in range(2):
                kt = k[:, i * LANES:(i + 1) * LANES].T
                for p, at, src in spots:
                    kt_v[2 * c + i, p, :, at:at + rows] = kt[:, src:src + rows]

    get_wuk.wait()
    get_wuv.wait()
    for t in sorted(range(chips), key=lambda t: min(t, chips - t)):
        for d in range(2):
            if t > 0:
                arrived(2 * lax.rem(my_chip + t, chips) + d)
        if t == 0:
            arrived(me + 1 - 2 * lax.rem(me, 2))
        up_project(t)

    factor = (nope + rope) ** -0.5 * math.log2(math.e)
    steps = pairs // GROUP

    def scores(g):
        for i in range(GROUP):
            p = g * GROUP + i
            early = jnp.concatenate([kt_v[p, 0], krt_v[0]], axis=0)
            late = jnp.concatenate([kt_v[p, 1], krt_v[1]], axis=0)
            s_v[g % 2, i, :count] = mm(qcat[p], early) * factor + bias_v[:count]
            s_v[g % 2, i, count:] = mm(qcat[p, rows:], late) * factor + bias_v[count:]

    def halves(a, op):
        return op(a[:, :LANES], a[:, LANES:])

    def weights(g):
        for i in range(GROUP):
            a, b, c = s_v[g % 2, i, :rows], s_v[g % 2, i, rows:count], s_v[g % 2, i, count:]
            m_a = jnp.max(halves(a, jnp.maximum), axis=1, keepdims=True)
            m_b = jnp.max(jnp.maximum(halves(b, jnp.maximum), halves(c, jnp.maximum)), axis=1, keepdims=True)
            a, b, c = jnp.exp2(a - m_a), jnp.exp2(b - m_b), jnp.exp2(c - m_b)
            p_v[g % 2, i, :rows] = a.astype(jnp.bfloat16)
            p_v[g % 2, i, rows:count] = b.astype(jnp.bfloat16)
            p_v[g % 2, i, count:] = c.astype(jnp.bfloat16)
            l_a = jnp.sum(halves(a, jnp.add), axis=1, keepdims=True)
            l_b = jnp.sum(halves(b, jnp.add) + halves(c, jnp.add), axis=1, keepdims=True)
            l_v[g % 2, i, :rows] = jnp.broadcast_to(1.0 / l_a, (rows, LANES))
            l_v[g % 2, i, rows:] = jnp.broadcast_to(1.0 / l_b, (rows, LANES))

    def values(g):
        for i in range(GROUP):
            cols = slice((g * GROUP + i) * LANES, (g * GROUP + i + 1) * LANES)
            o = mm(p_v[g % 2, i, :count], v_v[0, :, cols])
            o_a = o[:rows] * l_v[g % 2, i, :rows]
            o_b = (o[rows:] + mm(p_v[g % 2, i, count:], v_v[1, :, cols])) * l_v[g % 2, i, rows:]
            o_v[:half, cols] = jnp.where(low[:half], o_a[:half], o_a[half:]).astype(jnp.bfloat16)
            o_v[half:, cols] = jnp.where(low[:half], o_b[:half], o_b[half:]).astype(jnp.bfloat16)

    for g in range(steps + 2):
        if g >= 2:
            values(g - 2)
        if 1 <= g <= steps:
            weights(g - 1)
        if g < steps:
            scores(g)

    for get in get_wout:
        get.wait()
    for c in range(OUT_CHUNKS):
        cols = slice(c * out_chunk, (c + 1) * out_chunk)
        y_v[:, cols] = mm(o_v[...], wout_v[:, cols]).astype(jnp.bfloat16)
    for k in range(n - 1):
        sent(k)


def solution(mesh):
    n = mesh.shape["ctx"]
    row_spec = P(("dp", "ctx"), None)
    id_spec = P(("dp", "ctx"))

    def per_device(x, pos, seg, w_dq, w_uq, w_qr, w_dkv, w_kr, w_uk, w_uv, w_out, gain_q, gain_kv):
        rows, width = x.shape
        pairs = w_uq.shape[1] // LANES
        keys = n * rows
        kv_rank = w_dkv.shape[1]
        bf, f32 = jnp.bfloat16, jnp.float32
        args = (x, pos.reshape(1, rows), w_dq, w_uq, w_qr, w_dkv, w_kr.T, w_uk, w_uv, w_out,
                gain_q, gain_kv)
        scratch = [pltpu.VMEM(a.shape, a.dtype) for a in args]
        scratch += [
            pltpu.VMEM((n, rows + PACK_ROWS, kv_rank), bf),
            pltpu.VMEM((rows, w_dq.shape[1]), bf),
            pltpu.VMEM((pairs, 2 * rows, 2 * LANES), bf),
            pltpu.VMEM((pairs, 2, LANES, keys // 2), bf),
            pltpu.VMEM((2, LANES, keys // 2), bf),
            pltpu.VMEM((2, keys // 2, w_uv.shape[1]), bf),
            pltpu.VMEM((3 * rows, keys // 2), f32),
            pltpu.VMEM((rows, w_uv.shape[1]), bf),
            pltpu.VMEM((2, GROUP, 3 * rows, keys // 2), f32),
            pltpu.VMEM((2, GROUP, 3 * rows, keys // 2), bf),
            pltpu.VMEM((2, GROUP, 2 * rows, LANES), f32),
            pltpu.SemaphoreType.DMA((len(args) - 1 + OUT_CHUNKS,)),
            pltpu.SemaphoreType.DMA((n - 1,)),
            pltpu.SemaphoreType.DMA((n,)),
        ]
        return pl.pallas_call(
            functools.partial(layer_kernel, n),
            out_shape=pltpu.VMEM(x.shape, bf),
            in_specs=[pl.BlockSpec(memory_space=pltpu.HBM)] * len(args),
            out_specs=pl.BlockSpec(memory_space=pltpu.VMEM),
            scratch_shapes=scratch,
            compiler_params=pltpu.CompilerParams(collective_id=0, has_side_effects=True, vmem_limit_bytes=62000000),
        )(*args)

    return jax.shard_map(per_device, mesh=mesh, in_specs=(row_spec, id_spec, id_spec) + (P(),) * 10, out_specs=row_spec, check_vma=False)
```

time: 18.3 us -> 16.8 us (0.918)
  Pallas kernels: 17.5 us -> 16 us
    pallas_call x1, Pallas kernels: 17.5 us -> 16 us  [per_device(): pl.pallas_call(functools.partial(layer_kernel, n), out_shape=pltpu.VMEM(x...]
where the time goes in v6:
time: 16.8 us; the launch traced here: 16.7 us
  Pallas kernels  16 us (95%)
  local copies, waits for them, and re-layouts  0.73 us (4%)
    pallas_call x1, Pallas kernels, per_device(): pl.pallas_call(functools.partial(layer_kernel, n), out_shape=pltpu.VMEM(x...  16 us
    unnamed x1, local copies, waits for them, and re-layouts  0.73 us

profile of v6, /device:TPU:112, one launch (start us, length us, event | category | flops | bytes accessed | tf_op | source)
XLA Modules:
  0.0 16.7 jit_solution(9365680158658377731)
XLA Ops:
  0.0 16.0 %shard_map.118 = bf16[64,2560]{1,0:T(8,128)(2,1)S(1)} custom-call(bf16[64,2560]{1,0:T(8,128)(2,1)} %x_h.1, s32[1,64]{1,0:T(1,128)} %bitcast.3, bf16[2560,768]{1,0:T(8,128)(2,1)} %wdq_h.1, bf16[768,2560]{1,0:T(8,128)(2,1)} %wuq_h.1, bf16[768,1280]{1,0:T(8,128)(2,1)} %wqr_h.1, bf16[2560,256]{1,0:T(8,128)(2,1)} %wdkv_h.1, bf16[32,2560]{1,0:T(8,128)(2,1)} %bitcast.2, ...), custom_call_target="tpu_custom_call" | custom-call | tf_op jit(solution)/shard_map/pallas_call | solution.py:335
  16.0 0.7 %copy.14 = bf16[64,2560]{1,0:T(8,128)(2,1)} copy(bf16[64,2560]{1,0:T(8,128)(2,1)S(1)} %shard_map.118) | data formatting | bytes 655360

commit v7 on v6

--- a/solution.py
+++ b/solution.py
@@ -15,6 +15,7 @@
 PACK_ROWS = 16
 GROUP = 2
 OUT_CHUNKS = 5
+KV_CUTS = (0, 3, 6, 8, 10)
 MESH = pl.DeviceIdType.MESH
 NT = (((1,), (1,)), ((), ()))
 
@@ -34,7 +35,7 @@
 
 def layer_kernel(n, x_h, pos_h, wdq_h, wuq_h, wqr_h, wdkv_h, wkr_h, wuk_h, wuv_h, wout_h, gq_h, gkv_h, y_v,
                  x_v, pos_v, wdq_v, wuq_v, wqr_v, wdkv_v, wkr_v, wuk_v, wuv_v, wout_v, gq_v, gkv_v,
-                 lat, cq_v, qcat, kt_v, krt_v, v_v, bias_v, o_v, s_v, p_v, l_v, in_sem, send_sem, recv_sem):
+                 lat, kv_v, cq_v, qcat, kt_v, krt_v, v_v, bias_v, o_v, s_v, p_v, l_v, in_sem, send_sem, recv_sem):
     rows, width = x_v.shape
     kv_rank = wdkv_v.shape[1]
     rope = wkr_v.shape[0]
@@ -49,11 +50,11 @@
 
     me = lax.axis_index("ctx")
     my_chip = me // 2
-    peers = [lax.rem(me + k, n) for k in range(1, n)]
-
-    barrier = pltpu.get_barrier_semaphore()
-    for peer in peers:
-        pl.semaphore_signal(barrier, inc=1, device_id={"ctx": peer}, device_id_type=MESH)
+    peers = [jnp.where(me > k, k, k + 1) for k in range(n - 1)]
+
+    def chip_at(slot):
+        return jnp.where(slot == 0, my_chip, jnp.where(slot > my_chip, slot, slot - 1))
+
 
     fetches = []
 
@@ -68,7 +69,9 @@
     get_pos = fetch(pos_h, pos_v)
     get_x = fetch(x_h, x_v)
     get_wkr = fetch(wkr_h, wkr_v)
-    get_wdkv = fetch(wdkv_h, wdkv_v)
+    depth = 2 * LANES
+    cuts = [width // depth * c // 10 * depth for c in KV_CUTS]
+    get_wdkv = [fetch(wdkv_h.at[pl.ds(lo, hi - lo)], wdkv_v.at[pl.ds(lo, hi - lo)]) for lo, hi in zip(cuts[::2], cuts[2::2])]
     get_gkv = fetch(gkv_h, gkv_v)
     get_gq = fetch(gq_h, gq_v)
     get_wdq = fetch(wdq_h, wdq_v)
@@ -78,9 +81,14 @@
     get_wuv = fetch(wuv_h, wuv_v)
     get_wout = [fetch(wout_h.at[:, pl.ds(c * out_chunk, out_chunk)], wout_v.at[:, pl.ds(c * out_chunk, out_chunk)])
                 for c in range(OUT_CHUNKS)]
-    start(get_pos, get_x, get_wkr, get_wdkv, get_gkv, get_gq, get_wdq)
+    start(get_pos, get_x, get_wkr, get_gkv, *get_wdkv)
+
+    barrier = pltpu.get_barrier_semaphore()
+    for peer in peers:
+        pl.semaphore_signal(barrier, inc=1, device_id={"ctx": peer}, device_id_type=MESH)
 
     get_pos.wait()
+    start(get_gq, get_wdq)
     pos_row = pos_v[...].astype(jnp.float32)
 
     def pos_of(count, index):
@@ -113,7 +121,7 @@
     inner = lax.rem(col, rows)
 
     def key_seq(slot, late):
-        dev = 2 * lax.rem(my_chip + slot, chips) + inner // half
+        dev = 2 * chip_at(slot) + inner // half
         return half * jnp.where(late, 2 * n - 1 - dev, dev) + lax.rem(inner, half)
 
     def visible(seq, lo, hi):
@@ -121,18 +129,16 @@
 
     bias_v[:count] = visible(key_seq(slot, False), q_first, q_seq)
     bias_v[count:] = visible(key_seq(swapped, True), q_first[rows:], q_seq[rows:])
-
-    for peer in peers:
-        @pl.when(peer < me)
-        def _():
-            lat[peer, short:, :] = jnp.zeros((half, kv_rank), jnp.bfloat16)
 
     get_x.wait()
     get_wkr.wait()
     kr = mm(x_v[...], wkr_v[...], NT)
-    get_wdkv.wait()
+    for c, get in enumerate(get_wdkv):
+        get.wait()
+        for i in range(2 * c, 2 * c + 2):
+            kv_v[i] = mm(x_v[:, cuts[i]:cuts[i + 1]], wdkv_v[cuts[i]:cuts[i + 1]])
+    kv = sum(kv_v[i] for i in range(len(cuts) - 1))
     start(get_wuq, get_wqr, get_wuk, get_wuv)
-    kv = mm(x_v[...], wdkv_v[...])
     get_gkv.wait()
     c_kv = rms_norm(kv, gkv_v[...].astype(jnp.float32).reshape(1, -1))
     lat[me, :half, :] = c_kv[:half]
@@ -147,40 +153,12 @@
 
     pl.semaphore_wait(barrier, n - 1)
 
-    def push(block, peer, index, count):
-        at = lat.at[block, pl.ds(0, count)]
-        return pltpu.make_async_remote_copy(src_ref=at, dst_ref=at, send_sem=send_sem.at[index],
+    def push(block, peer, index):
+        return pltpu.make_async_remote_copy(src_ref=lat.at[block], dst_ref=lat.at[block], send_sem=send_sem.at[index],
                                             recv_sem=recv_sem.at[block], device_id={"ctx": peer}, device_id_type=MESH)
 
-    def send(k):
-        @pl.when(peers[k] < me)
-        def _():
-            push(me, peers[k], k, short + half).start()
-
-        @pl.when(peers[k] > me)
-        def _():
-            push(me, peers[k], k, short).start()
-
-    def sent(k):
-        @pl.when(peers[k] < me)
-        def _():
-            push(me, peers[k], k, short + half).wait_send()
-
-        @pl.when(peers[k] > me)
-        def _():
-            push(me, peers[k], k, short).wait_send()
-
-    def arrived(block):
-        @pl.when(block > me)
-        def _():
-            push(block, me, 0, short + half).wait_recv()
-
-        @pl.when(block < me)
-        def _():
-            push(block, me, 0, short).wait_recv()
-
-    for k in sorted(range(n - 1), key=lambda k: -min(k + 1, n - 1 - k)):
-        send(k)
+    sends = [push(me, peer, k) for k, peer in enumerate(peers)]
+    start(*sends)
 
     get_gq.wait()
     get_wdq.wait()
@@ -214,7 +192,7 @@
     same = jnp.where(same, 1.0, 0.0).astype(jnp.bfloat16)
 
     def up_project(t):
-        chip = lax.rem(my_chip + t, chips)
+        chip = chip_at(t)
         block = lat[pl.ds(2 * chip, 2)]
         pieces = [block[:, :half].reshape(rows, kv_rank), block[:, short:].reshape(rows, kv_rank)]
         groups = half // PACK_ROWS
@@ -230,22 +208,22 @@
         for c in range(pairs // 2):
             cols = slice(c * 2 * LANES, (c + 1) * 2 * LANES)
             k = mm(c_chip, wuk_v[:, cols]).astype(jnp.bfloat16)
-            v = mm(c_chip, wuv_v[:, cols]).astype(jnp.bfloat16)
-            for p, at, src in spots:
-                v_v[p, at:at + rows, cols] = v[src:src + rows]
             for i in range(2):
                 kt = k[:, i * LANES:(i + 1) * LANES].T
                 for p, at, src in spots:
                     kt_v[2 * c + i, p, :, at:at + rows] = kt[:, src:src + rows]
+        for c in range(pairs // 2):
+            cols = slice(c * 2 * LANES, (c + 1) * 2 * LANES)
+            v = mm(c_chip, wuv_v[:, cols]).astype(jnp.bfloat16)
+            for p, at, src in spots:
+                v_v[p, at:at + rows, cols] = v[src:src + rows]
 
     get_wuk.wait()
     get_wuv.wait()
-    for t in sorted(range(chips), key=lambda t: min(t, chips - t)):
-        for d in range(2):
-            if t > 0:
-                arrived(2 * lax.rem(my_chip + t, chips) + d)
-        if t == 0:
-            arrived(me + 1 - 2 * lax.rem(me, 2))
+    for t in range(chips):
+        chip = chip_at(t)
+        for block in [2 * chip, 2 * chip + 1] if t else [me + 1 - 2 * lax.rem(me, 2)]:
+            push(block, me, 0).wait_recv()
         up_project(t)
 
     factor = (nope + rope) ** -0.5 * math.log2(math.e)
@@ -298,8 +276,8 @@
     for c in range(OUT_CHUNKS):
         cols = slice(c * out_chunk, (c + 1) * out_chunk)
         y_v[:, cols] = mm(o_v[...], wout_v[:, cols]).astype(jnp.bfloat16)
-    for k in range(n - 1):
-        sent(k)
+    for cp in sends:
+        cp.wait_send()
 
 
 def solution(mesh):
@@ -318,6 +296,7 @@
         scratch = [pltpu.VMEM(a.shape, a.dtype) for a in args]
         scratch += [
             pltpu.VMEM((n, rows + PACK_ROWS, kv_rank), bf),
+            pltpu.VMEM((len(KV_CUTS) - 1, rows, kv_rank), f32),
             pltpu.VMEM((rows, w_dq.shape[1]), bf),
             pltpu.VMEM((pairs, 2 * rows, 2 * LANES), bf),
             pltpu.VMEM((pairs, 2, LANES, keys // 2), bf),
@@ -328,7 +307,7 @@
             pltpu.VMEM((2, GROUP, 3 * rows, keys // 2), f32),
             pltpu.VMEM((2, GROUP, 3 * rows, keys // 2), bf),
             pltpu.VMEM((2, GROUP, 2 * rows, LANES), f32),
-            pltpu.SemaphoreType.DMA((len(args) - 1 + OUT_CHUNKS,)),
+            pltpu.SemaphoreType.DMA((len(args) - 2 + len(KV_CUTS) // 2 + OUT_CHUNKS,)),
             pltpu.SemaphoreType.DMA((n - 1,)),
             pltpu.SemaphoreType.DMA((n,)),
         ]

time: 16.8 us -> 16.1 us (0.958)
  the two profiles are of different devices: /device:TPU:112 before, /device:TPU:113 now
where the time goes in v7:
time: 16.1 us; the launch traced here: 16 us
  Pallas kernels  15.3 us (95%)
  local copies, waits for them, and re-layouts  0.73 us (5%)
    pallas_call x1, Pallas kernels, per_device(): pl.pallas_call(functools.partial(layer_kernel, n), out_shape=pltpu.VMEM(x...  15.3 us
    unnamed x1, local copies, waits for them, and re-layouts  0.73 us

profile of v7, /device:TPU:113, one launch (start us, length us, event | category | flops | bytes accessed | tf_op | source)
XLA Modules:
  0.0 16.0 jit_solution(17900955030561514431)
XLA Ops:
  0.0 15.3 %shard_map.118 = bf16[64,2560]{1,0:T(8,128)(2,1)S(1)} custom-call(bf16[64,2560]{1,0:T(8,128)(2,1)} %x_h.1, s32[1,64]{1,0:T(1,128)} %bitcast.3, bf16[2560,768]{1,0:T(8,128)(2,1)} %wdq_h.1, bf16[768,2560]{1,0:T(8,128)(2,1)} %wuq_h.1, bf16[768,1280]{1,0:T(8,128)(2,1)} %wqr_h.1, bf16[2560,256]{1,0:T(8,128)(2,1)} %wdkv_h.1, bf16[32,2560]{1,0:T(8,128)(2,1)} %bitcast.2, ...), custom_call_target="tpu_custom_call" | custom-call | tf_op jit(solution)/shard_map/pallas_call | solution.py:314
  15.3 0.7 %copy.14 = bf16[64,2560]{1,0:T(8,128)(2,1)} copy(bf16[64,2560]{1,0:T(8,128)(2,1)S(1)} %shard_map.118) | data formatting | bytes 655360

commit v8 on v7

--- a/solution.py
+++ b/solution.py
@@ -13,9 +13,9 @@
 MASKED = -1e30
 LANES = 128
 PACK_ROWS = 16
+PACKS = 2
 GROUP = 2
-OUT_CHUNKS = 5
-KV_CUTS = (0, 3, 6, 8, 10)
+KV_CUTS = (0, 5, 10)
 MESH = pl.DeviceIdType.MESH
 NT = (((1,), (1,)), ((), ()))
 
@@ -45,12 +45,13 @@
     half = rows // 2
     chips = n // 2
     keys = chips * rows
-    short = half + PACK_ROWS
-    out_chunk = width // OUT_CHUNKS
+    pack_rows = PACK_ROWS // PACKS
+    panels, _, panel = wout_v.shape
 
     me = lax.axis_index("ctx")
     my_chip = me // 2
-    peers = [jnp.where(me > k, k, k + 1) for k in range(n - 1)]
+    partner = me + 1 - 2 * lax.rem(me, 2)
+    odd = lax.rem(me, 2) == 1
 
     def chip_at(slot):
         return jnp.where(slot == 0, my_chip, jnp.where(slot > my_chip, slot, slot - 1))
@@ -71,7 +72,7 @@
     get_wkr = fetch(wkr_h, wkr_v)
     depth = 2 * LANES
     cuts = [width // depth * c // 10 * depth for c in KV_CUTS]
-    get_wdkv = [fetch(wdkv_h.at[pl.ds(lo, hi - lo)], wdkv_v.at[pl.ds(lo, hi - lo)]) for lo, hi in zip(cuts[::2], cuts[2::2])]
+    get_wdkv = [fetch(wdkv_h.at[pl.ds(lo, hi - lo)], wdkv_v.at[pl.ds(lo, hi - lo)]) for lo, hi in zip(cuts, cuts[1:])]
     get_gkv = fetch(gkv_h, gkv_v)
     get_gq = fetch(gq_h, gq_v)
     get_wdq = fetch(wdq_h, wdq_v)
@@ -79,15 +80,21 @@
     get_wqr = fetch(wqr_h, wqr_v)
     get_wuk = fetch(wuk_h, wuk_v)
     get_wuv = fetch(wuv_h, wuv_v)
-    get_wout = [fetch(wout_h.at[:, pl.ds(c * out_chunk, out_chunk)], wout_v.at[:, pl.ds(c * out_chunk, out_chunk)])
-                for c in range(OUT_CHUNKS)]
+    get_wout = [fetch(wout_h.at[:, pl.ds(c * panel, panel)], wout_v.at[c]) for c in range(panels)]
     start(get_pos, get_x, get_wkr, get_gkv, *get_wdkv)
 
     barrier = pltpu.get_barrier_semaphore()
-    for peer in peers:
-        pl.semaphore_signal(barrier, inc=1, device_id={"ctx": peer}, device_id_type=MESH)
+    pl.semaphore_signal(barrier, inc=1, device_id={"ctx": partner}, device_id_type=MESH)
+
+    @pl.when(odd)
+    def _():
+        for t in range(1, chips):
+            for d in range(2):
+                pl.semaphore_signal(barrier, inc=1, device_id={"ctx": 2 * chip_at(t) + d}, device_id_type=MESH)
 
     get_pos.wait()
+    get_x.wait()
+    get_wkr.wait()
     start(get_gq, get_wdq)
     pos_row = pos_v[...].astype(jnp.float32)
 
@@ -130,35 +137,41 @@
     bias_v[:count] = visible(key_seq(slot, False), q_first, q_seq)
     bias_v[count:] = visible(key_seq(swapped, True), q_first[rows:], q_seq[rows:])
 
-    get_x.wait()
-    get_wkr.wait()
     kr = mm(x_v[...], wkr_v[...], NT)
-    for c, get in enumerate(get_wdkv):
+    for get in get_wdkv:
         get.wait()
-        for i in range(2 * c, 2 * c + 2):
-            kv_v[i] = mm(x_v[:, cuts[i]:cuts[i + 1]], wdkv_v[cuts[i]:cuts[i + 1]])
-    kv = sum(kv_v[i] for i in range(len(cuts) - 1))
+    for i in range(kv_rank // LANES):
+        kv_v[:, i * LANES:(i + 1) * LANES] = mm(x_v[...], wdkv_v[:, i * LANES:(i + 1) * LANES])
+    kv = kv_v[...]
     start(get_wuq, get_wqr, get_wuk, get_wuv)
     get_gkv.wait()
     c_kv = rms_norm(kv, gkv_v[...].astype(jnp.float32).reshape(1, -1))
-    lat[me, :half, :] = c_kv[:half]
-    lat[me, short:, :] = c_kv[half:]
+    lat[me, :rows, :] = c_kv
     kr = rope_lanes(jnp.concatenate([kr] * (LANES // rope), axis=1))
-    packed = jnp.zeros((PACK_ROWS, LANES), jnp.bfloat16)
+    packed = jnp.zeros((PACK_ROWS, LANES), jnp.float32)
+    kr = kr.astype(jnp.float32)
     part = iota((PACK_ROWS, LANES), 1) // rope
     for s in range(rows // PACK_ROWS):
         packed = jnp.where(part == s, kr[s * PACK_ROWS:(s + 1) * PACK_ROWS], packed)
-    lat[me, half:short, :LANES] = packed
-    lat[me, half:short, LANES:] = jnp.zeros((PACK_ROWS, kv_rank - LANES), jnp.bfloat16)
-
-    pl.semaphore_wait(barrier, n - 1)
+    for i in range(PACKS):
+        lat[me, rows:, i * LANES:(i + 1) * LANES] = packed[i * pack_rows:(i + 1) * pack_rows].astype(jnp.bfloat16)
+
+    pl.semaphore_wait(barrier, chips)
 
     def push(block, peer, index):
         return pltpu.make_async_remote_copy(src_ref=lat.at[block], dst_ref=lat.at[block], send_sem=send_sem.at[index],
                                             recv_sem=recv_sem.at[block], device_id={"ctx": peer}, device_id_type=MESH)
 
-    sends = [push(me, peer, k) for k, peer in enumerate(peers)]
+    sends = [push(me, 2 * chip_at(t) + 1, t) for t in range(1, chips)] + [push(me, partner, 0)]
     start(*sends)
+
+    def forward(t):
+        return [push(2 * chip_at(t) + d, partner, chips + 2 * (t - 1) + d) for d in range(2)]
+
+    def relay(t):
+        for d, cp in enumerate(forward(t)):
+            push(2 * chip_at(t) + d, me, 0).wait_recv()
+            cp.start()
 
     get_gq.wait()
     get_wdq.wait()
@@ -193,10 +206,12 @@
 
     def up_project(t):
         chip = chip_at(t)
-        block = lat[pl.ds(2 * chip, 2)]
-        pieces = [block[:, :half].reshape(rows, kv_rank), block[:, short:].reshape(rows, kv_rank)]
+        block = lat[pl.ds(2 * chip, 2), :rows]
+        pieces = [block[:, :half].reshape(rows, kv_rank), block[:, half:rows].reshape(rows, kv_rank)]
         groups = half // PACK_ROWS
-        spread = [[jnp.where(part == p * groups + s, block[d, half:short, :LANES], jnp.zeros((PACK_ROWS, LANES), jnp.bfloat16))
+        tails = [lat[2 * chip + d, rows:].astype(jnp.float32) for d in range(2)]
+        packs = [jnp.concatenate([a[:, i * LANES:(i + 1) * LANES] for i in range(PACKS)], axis=0) for a in tails]
+        spread = [[jnp.where(part == p * groups + s, packs[d], 0.0).astype(jnp.bfloat16)
                    for d in range(2) for s in range(groups)] for p in range(2)]
         first_piece = t % 2
         order = [first_piece, 1 - first_piece]
@@ -215,15 +230,25 @@
         for c in range(pairs // 2):
             cols = slice(c * 2 * LANES, (c + 1) * 2 * LANES)
             v = mm(c_chip, wuv_v[:, cols]).astype(jnp.bfloat16)
-            for p, at, src in spots:
-                v_v[p, at:at + rows, cols] = v[src:src + rows]
+            for i in range(2):
+                for p, at, src in spots:
+                    v_v[2 * c + i, p, at:at + rows] = v[src:src + rows, i * LANES:(i + 1) * LANES]
 
     get_wuk.wait()
     get_wuv.wait()
     for t in range(chips):
-        chip = chip_at(t)
-        for block in [2 * chip, 2 * chip + 1] if t else [me + 1 - 2 * lax.rem(me, 2)]:
-            push(block, me, 0).wait_recv()
+        for first_slot, last_slot in [(1, 2)] * (t == 0) + [(2, chips)] * (t == 2):
+            @pl.when(odd)
+            def _():
+                for u in range(first_slot, last_slot):
+                    relay(u)
+        if t == 0:
+            push(partner, me, 0).wait_recv()
+        else:
+            @pl.when(jnp.logical_not(odd))
+            def _():
+                for d in range(2):
+                    push(2 * chip_at(t) + d, me, 0).wait_recv()
         up_project(t)
 
     factor = (nope + rope) ** -0.5 * math.log2(math.e)
@@ -257,9 +282,9 @@
     def values(g):
         for i in range(GROUP):
             cols = slice((g * GROUP + i) * LANES, (g * GROUP + i + 1) * LANES)
-            o = mm(p_v[g % 2, i, :count], v_v[0, :, cols])
+            o = mm(p_v[g % 2, i, :count], v_v[g * GROUP + i, 0])
             o_a = o[:rows] * l_v[g % 2, i, :rows]
-            o_b = (o[rows:] + mm(p_v[g % 2, i, count:], v_v[1, :, cols])) * l_v[g % 2, i, rows:]
+            o_b = (o[rows:] + mm(p_v[g % 2, i, count:], v_v[g * GROUP + i, 1])) * l_v[g % 2, i, rows:]
             o_v[:half, cols] = jnp.where(low[:half], o_a[:half], o_a[half:]).astype(jnp.bfloat16)
             o_v[half:, cols] = jnp.where(low[:half], o_b[:half], o_b[half:]).astype(jnp.bfloat16)
 
@@ -273,11 +298,16 @@
 
     for get in get_wout:
         get.wait()
-    for c in range(OUT_CHUNKS):
-        cols = slice(c * out_chunk, (c + 1) * out_chunk)
-        y_v[:, cols] = mm(o_v[...], wout_v[:, cols]).astype(jnp.bfloat16)
+    for c in range(panels):
+        y_v[:, c * panel:(c + 1) * panel] = mm(o_v[...], wout_v[c]).astype(jnp.bfloat16)
     for cp in sends:
         cp.wait_send()
+
+    @pl.when(odd)
+    def _():
+        for t in range(1, chips):
+            for cp in forward(t):
+                cp.wait_send()
 
 
 def solution(mesh):
@@ -293,22 +323,23 @@
         bf, f32 = jnp.bfloat16, jnp.float32
         args = (x, pos.reshape(1, rows), w_dq, w_uq, w_qr, w_dkv, w_kr.T, w_uk, w_uv, w_out,
                 gain_q, gain_kv)
-        scratch = [pltpu.VMEM(a.shape, a.dtype) for a in args]
+        panels = w_out.shape[1] // (2 * LANES)
+        scratch = [pltpu.VMEM((panels, w_out.shape[0], 2 * LANES) if a is w_out else a.shape, a.dtype) for a in args]
         scratch += [
-            pltpu.VMEM((n, rows + PACK_ROWS, kv_rank), bf),
-            pltpu.VMEM((len(KV_CUTS) - 1, rows, kv_rank), f32),
+            pltpu.VMEM((n, rows + PACK_ROWS // PACKS, kv_rank), bf),
+            pltpu.VMEM((rows, kv_rank), f32),
             pltpu.VMEM((rows, w_dq.shape[1]), bf),
             pltpu.VMEM((pairs, 2 * rows, 2 * LANES), bf),
             pltpu.VMEM((pairs, 2, LANES, keys // 2), bf),
             pltpu.VMEM((2, LANES, keys // 2), bf),
-            pltpu.VMEM((2, keys // 2, w_uv.shape[1]), bf),
+            pltpu.VMEM((pairs, 2, keys // 2, LANES), bf),
             pltpu.VMEM((3 * rows, keys // 2), f32),
             pltpu.VMEM((rows, w_uv.shape[1]), bf),
             pltpu.VMEM((2, GROUP, 3 * rows, keys // 2), f32),
             pltpu.VMEM((2, GROUP, 3 * rows, keys // 2), bf),
             pltpu.VMEM((2, GROUP, 2 * rows, LANES), f32),
-            pltpu.SemaphoreType.DMA((len(args) - 2 + len(KV_CUTS) // 2 + OUT_CHUNKS,)),
-            pltpu.SemaphoreType.DMA((n - 1,)),
+            pltpu.SemaphoreType.DMA((len(args) - 2 + len(KV_CUTS) - 1 + panels,)),
+            pltpu.SemaphoreType.DMA((n // 2 + n - 2,)),
             pltpu.SemaphoreType.DMA((n,)),
         ]
         return pl.pallas_call(

time: 16.1 us -> 15.1 us (0.938)
  the two profiles are of different devices: /device:TPU:113 before, /device:TPU:112 now
where the time goes in v8:
time: 15.1 us
  Pallas kernels  14.3 us (95%)
  local copies, waits for them, and re-layouts  0.73 us (5%)
    pallas_call x1, Pallas kernels, per_device(): pl.pallas_call(functools.partial(layer_kernel, n), out_shape=pltpu.VMEM(x...  14.3 us
    unnamed x1, local copies, waits for them, and re-layouts  0.73 us

profile of v8, /device:TPU:112, one launch (start us, length us, event | category | flops | bytes accessed | tf_op | source)
XLA Modules:
  0.0 15.1 jit_solution(5570974560759611672)
XLA Ops:
  0.0 14.3 %shard_map.118 = bf16[64,2560]{1,0:T(8,128)(2,1)S(1)} custom-call(bf16[64,2560]{1,0:T(8,128)(2,1)} %x_h.1, s32[1,64]{1,0:T(1,128)} %bitcast.3, bf16[2560,768]{1,0:T(8,128)(2,1)} %wdq_h.1, bf16[768,2560]{1,0:T(8,128)(2,1)} %wuq_h.1, bf16[768,1280]{1,0:T(8,128)(2,1)} %wqr_h.1, bf16[2560,256]{1,0:T(8,128)(2,1)} %wdkv_h.1, bf16[32,2560]{1,0:T(8,128)(2,1)} %bitcast.2, ...), custom_call_target="tpu_custom_call" | custom-call | tf_op jit(solution)/shard_map/pallas_call | solution.py:345
  14.3 0.7 %copy.14 = bf16[64,2560]{1,0:T(8,128)(2,1)} copy(bf16[64,2560]{1,0:T(8,128)(2,1)S(1)} %shard_map.118) | data formatting | bytes 655360

commit v9 on v8

--- a/solution.py
+++ b/solution.py
@@ -14,8 +14,8 @@
 LANES = 128
 PACK_ROWS = 16
 PACKS = 2
-GROUP = 2
-KV_CUTS = (0, 5, 10)
+GROUP = 4
+KV_CUTS = (0, 2, 4, 6, 8, 10)
 MESH = pl.DeviceIdType.MESH
 NT = (((1,), (1,)), ((), ()))
 
@@ -35,7 +35,7 @@
 
 def layer_kernel(n, x_h, pos_h, wdq_h, wuq_h, wqr_h, wdkv_h, wkr_h, wuk_h, wuv_h, wout_h, gq_h, gkv_h, y_v,
                  x_v, pos_v, wdq_v, wuq_v, wqr_v, wdkv_v, wkr_v, wuk_v, wuv_v, wout_v, gq_v, gkv_v,
-                 lat, kv_v, cq_v, qcat, kt_v, krt_v, v_v, bias_v, o_v, s_v, p_v, l_v, in_sem, send_sem, recv_sem):
+                 lat, kv_v, cq_v, qcat, kt_v, krt_v, v_v, bias_v, o_v, s_v, p_v, l_v, y_sum, in_sem, send_sem, recv_sem):
     rows, width = x_v.shape
     kv_rank = wdkv_v.shape[1]
     rope = wkr_v.shape[0]
@@ -46,7 +46,9 @@
     chips = n // 2
     keys = chips * rows
     pack_rows = PACK_ROWS // PACKS
-    panels, _, panel = wout_v.shape
+    steps = pairs // GROUP
+    deep = GROUP * LANES
+    panel = 2 * LANES
 
     me = lax.axis_index("ctx")
     my_chip = me // 2
@@ -80,8 +82,8 @@
     get_wqr = fetch(wqr_h, wqr_v)
     get_wuk = fetch(wuk_h, wuk_v)
     get_wuv = fetch(wuv_h, wuv_v)
-    get_wout = [fetch(wout_h.at[:, pl.ds(c * panel, panel)], wout_v.at[c]) for c in range(panels)]
-    start(get_pos, get_x, get_wkr, get_gkv, *get_wdkv)
+    get_wout = [fetch(wout_h.at[pl.ds(g * deep, deep)], wout_v.at[pl.ds(g * deep, deep)]) for g in range(steps)]
+    start(get_pos, get_x, get_wkr, get_gkv, *get_wdkv, get_gq, get_wdq, get_wuq, get_wqr, get_wuk, get_wuv, *get_wout)
 
     barrier = pltpu.get_barrier_semaphore()
     pl.semaphore_signal(barrier, inc=1, device_id={"ctx": partner}, device_id_type=MESH)
@@ -95,7 +97,6 @@
     get_pos.wait()
     get_x.wait()
     get_wkr.wait()
-    start(get_gq, get_wdq)
     pos_row = pos_v[...].astype(jnp.float32)
 
     def pos_of(count, index):
@@ -143,7 +144,6 @@
     for i in range(kv_rank // LANES):
         kv_v[:, i * LANES:(i + 1) * LANES] = mm(x_v[...], wdkv_v[:, i * LANES:(i + 1) * LANES])
     kv = kv_v[...]
-    start(get_wuq, get_wqr, get_wuk, get_wuv)
     get_gkv.wait()
     c_kv = rms_norm(kv, gkv_v[...].astype(jnp.float32).reshape(1, -1))
     lat[me, :rows, :] = c_kv
@@ -175,7 +175,6 @@
 
     get_gq.wait()
     get_wdq.wait()
-    start(*get_wout)
     cq_v[...] = rms_norm(mm(x_v[...], wdq_v[...]), gq_v[...].astype(jnp.float32).reshape(1, -1))
     low = lane < nope
     zero = jnp.zeros((rows, LANES), jnp.bfloat16)
@@ -204,55 +203,59 @@
     same = lax.rem(iota((LANES, LANES), 0), rope) == lax.rem(iota((LANES, LANES), 1), rope)
     same = jnp.where(same, 1.0, 0.0).astype(jnp.bfloat16)
 
-    def up_project(t):
-        chip = chip_at(t)
-        block = lat[pl.ds(2 * chip, 2), :rows]
-        pieces = [block[:, :half].reshape(rows, kv_rank), block[:, half:rows].reshape(rows, kv_rank)]
+    def up_project(slots):
+        pieces, packs = [], []
         groups = half // PACK_ROWS
-        tails = [lat[2 * chip + d, rows:].astype(jnp.float32) for d in range(2)]
-        packs = [jnp.concatenate([a[:, i * LANES:(i + 1) * LANES] for i in range(PACKS)], axis=0) for a in tails]
-        spread = [[jnp.where(part == p * groups + s, packs[d], 0.0).astype(jnp.bfloat16)
-                   for d in range(2) for s in range(groups)] for p in range(2)]
-        first_piece = t % 2
-        order = [first_piece, 1 - first_piece]
-        c_chip = jnp.concatenate([pieces[p] for p in order], axis=0)
-        krt = mm(same, jnp.concatenate(spread[order[0]] + spread[order[1]], axis=0), NT).astype(jnp.bfloat16)
-        spots = [(order[i], (t - t % 2 + i) * rows, i * rows) for i in range(2)]
+        for t in slots:
+            chip = chip_at(t)
+            block = lat[pl.ds(2 * chip, 2), :rows]
+            tails = [lat[2 * chip + d, rows:].astype(jnp.float32) for d in range(2)]
+            tails = [jnp.concatenate([a[:, i * LANES:(i + 1) * LANES] for i in range(PACKS)], axis=0) for a in tails]
+            for p in [t % 2, 1 - t % 2]:
+                pieces.append(block[:, p * half:(p + 1) * half].reshape(rows, kv_rank))
+                packs += [jnp.where(part == p * groups + s, tails[d], 0.0).astype(jnp.bfloat16) for d in range(2) for s in range(groups)]
+        c_all = jnp.concatenate(pieces, axis=0)
+        krt = mm(same, jnp.concatenate(packs, axis=0), NT).astype(jnp.bfloat16)
+        spots = [((t + i) % 2, (t - t % 2 + i) * rows, (2 * j + i) * rows) for j, t in enumerate(slots) for i in range(2)]
         for p, at, src in spots:
             krt_v[p, :, at:at + rows] = krt[:, src:src + rows]
         for c in range(pairs // 2):
             cols = slice(c * 2 * LANES, (c + 1) * 2 * LANES)
-            k = mm(c_chip, wuk_v[:, cols]).astype(jnp.bfloat16)
+            k = mm(c_all, wuk_v[:, cols]).astype(jnp.bfloat16)
             for i in range(2):
                 kt = k[:, i * LANES:(i + 1) * LANES].T
                 for p, at, src in spots:
                     kt_v[2 * c + i, p, :, at:at + rows] = kt[:, src:src + rows]
         for c in range(pairs // 2):
             cols = slice(c * 2 * LANES, (c + 1) * 2 * LANES)
-            v = mm(c_chip, wuv_v[:, cols]).astype(jnp.bfloat16)
+            v = mm(c_all, wuv_v[:, cols]).astype(jnp.bfloat16)
             for i in range(2):
                 for p, at, src in spots:
                     v_v[2 * c + i, p, at:at + rows] = v[src:src + rows, i * LANES:(i + 1) * LANES]
 
     get_wuk.wait()
     get_wuv.wait()
-    for t in range(chips):
-        for first_slot, last_slot in [(1, 2)] * (t == 0) + [(2, chips)] * (t == 2):
-            @pl.when(odd)
-            def _():
-                for u in range(first_slot, last_slot):
-                    relay(u)
-        if t == 0:
-            push(partner, me, 0).wait_recv()
-        else:
-            @pl.when(jnp.logical_not(odd))
-            def _():
+    push(partner, me, 0).wait_recv()
+    for t in range(0, chips, 2):
+        slots = [u for u in (t, t + 1) if u > 0]
+
+        @pl.when(odd)
+        def _():
+            for u in slots:
+                relay(u)
+
+        @pl.when(jnp.logical_not(odd))
+        def _():
+            for u in slots:
                 for d in range(2):
-                    push(2 * chip_at(t) + d, me, 0).wait_recv()
-        up_project(t)
+                    push(2 * chip_at(u) + d, me, 0).wait_recv()
+
+        if t + 2 >= chips:
+            for get in get_wout:
+                get.wait()
+        up_project([t, t + 1])
 
     factor = (nope + rope) ** -0.5 * math.log2(math.e)
-    steps = pairs // GROUP
 
     def scores(g):
         for i in range(GROUP):
@@ -288,18 +291,26 @@
             o_v[:half, cols] = jnp.where(low[:half], o_a[:half], o_a[half:]).astype(jnp.bfloat16)
             o_v[half:, cols] = jnp.where(low[:half], o_b[:half], o_b[half:]).astype(jnp.bfloat16)
 
-    for g in range(steps + 2):
-        if g >= 2:
+    def project(g):
+        for c in range(width // panel):
+            cols = slice(c * panel, (c + 1) * panel)
+            y = mm(o_v[:, g * deep:(g + 1) * deep], wout_v[g * deep:(g + 1) * deep, cols])
+            if g > 0:
+                y += y_sum[:, cols]
+            if g + 1 < steps:
+                y_sum[:, cols] = y
+            else:
+                y_v[:, cols] = y.astype(jnp.bfloat16)
+
+    for g in range(steps + 3):
+        if g >= 3:
+            project(g - 3)
+        if 2 <= g < steps + 2:
             values(g - 2)
         if 1 <= g <= steps:
             weights(g - 1)
         if g < steps:
             scores(g)
-
-    for get in get_wout:
-        get.wait()
-    for c in range(panels):
-        y_v[:, c * panel:(c + 1) * panel] = mm(o_v[...], wout_v[c]).astype(jnp.bfloat16)
     for cp in sends:
         cp.wait_send()
 
@@ -323,8 +334,7 @@
         bf, f32 = jnp.bfloat16, jnp.float32
         args = (x, pos.reshape(1, rows), w_dq, w_uq, w_qr, w_dkv, w_kr.T, w_uk, w_uv, w_out,
                 gain_q, gain_kv)
-        panels = w_out.shape[1] // (2 * LANES)
-        scratch = [pltpu.VMEM((panels, w_out.shape[0], 2 * LANES) if a is w_out else a.shape, a.dtype) for a in args]
+        scratch = [pltpu.VMEM(a.shape, a.dtype) for a in args]
         scratch += [
             pltpu.VMEM((n, rows + PACK_ROWS // PACKS, kv_rank), bf),
             pltpu.VMEM((rows, kv_rank), f32),
@@ -338,7 +348,8 @@
             pltpu.VMEM((2, GROUP, 3 * rows, keys // 2), f32),
             pltpu.VMEM((2, GROUP, 3 * rows, keys // 2), bf),
             pltpu.VMEM((2, GROUP, 2 * rows, LANES), f32),
-            pltpu.SemaphoreType.DMA((len(args) - 2 + len(KV_CUTS) - 1 + panels,)),
+            pltpu.VMEM((rows, width), f32),
+            pltpu.SemaphoreType.DMA((len(args) - 2 + len(KV_CUTS) - 1 + pairs // GROUP,)),
             pltpu.SemaphoreType.DMA((n // 2 + n - 2,)),
             pltpu.SemaphoreType.DMA((n,)),
         ]

time: 15.1 us -> 14.9 us (0.987)
  Pallas kernels: 14.3 us -> 14.1 us
    pallas_call x1, Pallas kernels: 14.3 us -> 14.1 us  [per_device(): pl.pallas_call(functools.partial(layer_kernel, n), out_shape=pltpu.VMEM(x...]
where the time goes in v9:
time: 14.9 us; the launch traced here: 14.8 us
  Pallas kernels  14.1 us (95%)
  local copies, waits for them, and re-layouts  0.73 us (5%)
    pallas_call x1, Pallas kernels, per_device(): pl.pallas_call(functools.partial(layer_kernel, n), out_shape=pltpu.VMEM(x...  14.1 us
    unnamed x1, local copies, waits for them, and re-layouts  0.73 us

profile of v9, /device:TPU:112, one launch (start us, length us, event | category | flops | bytes accessed | tf_op | source)
XLA Modules:
  0.0 14.8 jit_solution(774305374020949069)
XLA Ops:
  0.0 14.1 %shard_map.118 = bf16[64,2560]{1,0:T(8,128)(2,1)S(1)} custom-call(bf16[64,2560]{1,0:T(8,128)(2,1)} %x_h.1, s32[1,64]{1,0:T(1,128)} %bitcast.3, bf16[2560,768]{1,0:T(8,128)(2,1)} %wdq_h.1, bf16[768,2560]{1,0:T(8,128)(2,1)} %wuq_h.1, bf16[768,1280]{1,0:T(8,128)(2,1)} %wqr_h.1, bf16[2560,256]{1,0:T(8,128)(2,1)} %wdkv_h.1, bf16[32,2560]{1,0:T(8,128)(2,1)} %bitcast.2, ...), custom_call_target="tpu_custom_call" | custom-call | tf_op jit(solution)/shard_map/pallas_call | solution.py:356
  14.1 0.7 %copy.14 = bf16[64,2560]{1,0:T(8,128)(2,1)} copy(bf16[64,2560]{1,0:T(8,128)(2,1)S(1)} %shard_map.118) | data formatting | bytes 655360

commit v10 on v9

--- a/solution.py
+++ b/solution.py
@@ -250,9 +250,6 @@
                 for d in range(2):
                     push(2 * chip_at(u) + d, me, 0).wait_recv()
 
-        if t + 2 >= chips:
-            for get in get_wout:
-                get.wait()
         up_project([t, t + 1])
 
     factor = (nope + rope) ** -0.5 * math.log2(math.e)
@@ -303,6 +300,9 @@
                 y_v[:, cols] = y.astype(jnp.bfloat16)
 
     for g in range(steps + 3):
+        if g == 3:
+            for get in get_wout:
+                get.wait()
         if g >= 3:
             project(g - 3)
         if 2 <= g < steps + 2:

time: 14.9 us -> 14.9 us (level)
  no operation moved by 1% of the time
where the time goes in v10:
time: 14.9 us
  Pallas kernels  14.1 us (95%)
  local copies, waits for them, and re-layouts  0.73 us (5%)
    pallas_call x1, Pallas kernels, per_device(): pl.pallas_call(functools.partial(layer_kernel, n), out_shape=pltpu.VMEM(x...  14.1 us
    unnamed x1, local copies, waits for them, and re-layouts  0.73 us

profile of v10, /device:TPU:112, one launch (start us, length us, event | category | flops | bytes accessed | tf_op | source)
XLA Modules:
  0.0 14.9 jit_solution(8697440662834147388)
XLA Ops:
  0.0 14.1 %shard_map.118 = bf16[64,2560]{1,0:T(8,128)(2,1)S(1)} custom-call(bf16[64,2560]{1,0:T(8,128)(2,1)} %x_h.1, s32[1,64]{1,0:T(1,128)} %bitcast.3, bf16[2560,768]{1,0:T(8,128)(2,1)} %wdq_h.1, bf16[768,2560]{1,0:T(8,128)(2,1)} %wuq_h.1, bf16[768,1280]{1,0:T(8,128)(2,1)} %wqr_h.1, bf16[2560,256]{1,0:T(8,128)(2,1)} %wdkv_h.1, bf16[32,2560]{1,0:T(8,128)(2,1)} %bitcast.2, ...), custom_call_target="tpu_custom_call" | custom-call | tf_op jit(solution)/shard_map/pallas_call | solution.py:356
  14.1 0.7 %copy.14 = bf16[64,2560]{1,0:T(8,128)(2,1)} copy(bf16[64,2560]{1,0:T(8,128)(2,1)S(1)} %shard_map.118) | data formatting | bytes 655360

commit v11 on v10

--- a/solution.py
+++ b/solution.py
@@ -198,9 +198,9 @@
         for i in range(2):
             t = rope_lanes(q[:, i * LANES:(i + 1) * LANES])
             for s in range(per):
-                put_query((c * 2 + i) * per + s, slice(LANES, 2 * LANES), jnp.where(lane // rope == s, t, zero))
-
-    same = lax.rem(iota((LANES, LANES), 0), rope) == lax.rem(iota((LANES, LANES), 1), rope)
+                put_query((c * 2 + i) * per + s, slice(LANES, LANES + rope), t[:, s * rope:(s + 1) * rope])
+
+    same = iota((rope, LANES), 0) == lax.rem(iota((rope, LANES), 1), rope)
     same = jnp.where(same, 1.0, 0.0).astype(jnp.bfloat16)
 
     def up_project(slots):
@@ -235,22 +235,24 @@
 
     get_wuk.wait()
     get_wuv.wait()
+    def receive(t):
+        for d in range(2):
+            push(2 * chip_at(t) + d, me, 0).wait_recv()
+
+    even = jnp.logical_not(odd)
     push(partner, me, 0).wait_recv()
-    for t in range(0, chips, 2):
-        slots = [u for u in (t, t + 1) if u > 0]
-
-        @pl.when(odd)
-        def _():
-            for u in slots:
-                relay(u)
-
-        @pl.when(jnp.logical_not(odd))
-        def _():
-            for u in slots:
-                for d in range(2):
-                    push(2 * chip_at(u) + d, me, 0).wait_recv()
-
-        up_project([t, t + 1])
+    pl.when(odd)(lambda: relay(1))
+    pl.when(even)(lambda: receive(1))
+    up_project([0, 1])
+
+    @pl.when(odd)
+    def _():
+        for t in range(2, chips):
+            relay(t)
+
+    for t in range(2, chips):
+        pl.when(even)(functools.partial(receive, t))
+        up_project([t])
 
     factor = (nope + rope) ** -0.5 * math.log2(math.e)
 
@@ -331,6 +333,7 @@
         pairs = w_uq.shape[1] // LANES
         keys = n * rows
         kv_rank = w_dkv.shape[1]
+        rope = w_kr.shape[1]
         bf, f32 = jnp.bfloat16, jnp.float32
         args = (x, pos.reshape(1, rows), w_dq, w_uq, w_qr, w_dkv, w_kr.T, w_uk, w_uv, w_out,
                 gain_q, gain_kv)
@@ -339,9 +342,9 @@
             pltpu.VMEM((n, rows + PACK_ROWS // PACKS, kv_rank), bf),
             pltpu.VMEM((rows, kv_rank), f32),
             pltpu.VMEM((rows, w_dq.shape[1]), bf),
-            pltpu.VMEM((pairs, 2 * rows, 2 * LANES), bf),
+            pltpu.VMEM((pairs, 2 * rows, LANES + rope), bf),
             pltpu.VMEM((pairs, 2, LANES, keys // 2), bf),
-            pltpu.VMEM((2, LANES, keys // 2), bf),
+            pltpu.VMEM((2, rope, keys // 2), bf),
             pltpu.VMEM((pairs, 2, keys // 2, LANES), bf),
             pltpu.VMEM((3 * rows, keys // 2), f32),
             pltpu.VMEM((rows, w_uv.shape[1]), bf),

time: 14.9 us -> 14.7 us (0.987)
  Pallas kernels: 14.1 us -> 13.9 us
    pallas_call x1, Pallas kernels: 14.1 us -> 13.9 us  [per_device(): pl.pallas_call(functools.partial(layer_kernel, n), out_shape=pltpu.VMEM(x...]
where the time goes in v11:
time: 14.7 us; the launch traced here: 14.6 us
  Pallas kernels  13.9 us (95%)
  local copies, waits for them, and re-layouts  0.73 us (5%)
    pallas_call x1, Pallas kernels, per_device(): pl.pallas_call(functools.partial(layer_kernel, n), out_shape=pltpu.VMEM(x...  13.9 us
    unnamed x1, local copies, waits for them, and re-layouts  0.73 us

profile of v11, /device:TPU:112, one launch (start us, length us, event | category | flops | bytes accessed | tf_op | source)
XLA Modules:
  0.0 14.6 jit_solution(13428502955473071962)
XLA Ops:
  0.0 13.9 %shard_map.118 = bf16[64,2560]{1,0:T(8,128)(2,1)S(1)} custom-call(bf16[64,2560]{1,0:T(8,128)(2,1)} %x_h.1, s32[1,64]{1,0:T(1,128)} %bitcast.3, bf16[2560,768]{1,0:T(8,128)(2,1)} %wdq_h.1, bf16[768,2560]{1,0:T(8,128)(2,1)} %wuq_h.1, bf16[768,1280]{1,0:T(8,128)(2,1)} %wqr_h.1, bf16[2560,256]{1,0:T(8,128)(2,1)} %wdkv_h.1, bf16[32,2560]{1,0:T(8,128)(2,1)} %bitcast.2, ...), custom_call_target="tpu_custom_call" | custom-call | tf_op jit(solution)/shard_map/pallas_call | solution.py:359
  13.9 0.7 %copy.14 = bf16[64,2560]{1,0:T(8,128)(2,1)} copy(bf16[64,2560]{1,0:T(8,128)(2,1)S(1)} %shard_map.118) | data formatting | bytes 655360

commit v12 on v11

--- a/solution.py
+++ b/solution.py
@@ -35,7 +35,7 @@
 
 def layer_kernel(n, x_h, pos_h, wdq_h, wuq_h, wqr_h, wdkv_h, wkr_h, wuk_h, wuv_h, wout_h, gq_h, gkv_h, y_v,
                  x_v, pos_v, wdq_v, wuq_v, wqr_v, wdkv_v, wkr_v, wuk_v, wuv_v, wout_v, gq_v, gkv_v,
-                 lat, kv_v, cq_v, qcat, kt_v, krt_v, v_v, bias_v, o_v, s_v, p_v, l_v, y_sum, in_sem, send_sem, recv_sem):
+                 lat, kv_v, cq_v, qcat, kt_v, krt_v, v_v, bias_v, o_v, s_v, p_v, l_v, y_sum, fs_v, fp_v, fl_v, in_sem, send_sem, recv_sem):
     rows, width = x_v.shape
     kv_rank = wdkv_v.shape[1]
     rope = wkr_v.shape[0]
@@ -141,9 +141,11 @@
     kr = mm(x_v[...], wkr_v[...], NT)
     for get in get_wdkv:
         get.wait()
-    for i in range(kv_rank // LANES):
-        kv_v[:, i * LANES:(i + 1) * LANES] = mm(x_v[...], wdkv_v[:, i * LANES:(i + 1) * LANES])
-    kv = kv_v[...]
+    for i in range(2):
+        at = slice(i * width // 2, (i + 1) * width // 2)
+        kv_v[i] = mm(x_v[:, at], wdkv_v[at])
+    turn = lax.rem(me, 2)
+    kv = kv_v[turn] + kv_v[1 - turn]
     get_gkv.wait()
     c_kv = rms_norm(kv, gkv_v[...].astype(jnp.float32).reshape(1, -1))
     lat[me, :rows, :] = c_kv
@@ -235,60 +237,46 @@
 
     get_wuk.wait()
     get_wuv.wait()
-    def receive(t):
-        for d in range(2):
-            push(2 * chip_at(t) + d, me, 0).wait_recv()
-
-    even = jnp.logical_not(odd)
-    push(partner, me, 0).wait_recv()
-    pl.when(odd)(lambda: relay(1))
-    pl.when(even)(lambda: receive(1))
-    up_project([0, 1])
-
-    @pl.when(odd)
-    def _():
-        for t in range(2, chips):
-            relay(t)
-
-    for t in range(2, chips):
-        pl.when(even)(functools.partial(receive, t))
-        up_project([t])
-
     factor = (nope + rope) ** -0.5 * math.log2(math.e)
 
-    def scores(g):
+    def scores(g, part):
         for i in range(GROUP):
             p = g * GROUP + i
+            top = rows if part == "second" else 0
             early = jnp.concatenate([kt_v[p, 0], krt_v[0]], axis=0)
             late = jnp.concatenate([kt_v[p, 1], krt_v[1]], axis=0)
-            s_v[g % 2, i, :count] = mm(qcat[p], early) * factor + bias_v[:count]
+            s_v[g % 2, i, top:count] = mm(qcat[p, top:], early) * factor + bias_v[top:count]
             s_v[g % 2, i, count:] = mm(qcat[p, rows:], late) * factor + bias_v[count:]
 
     def halves(a, op):
         return op(a[:, :LANES], a[:, LANES:])
 
-    def weights(g):
+    def weights(g, part):
         for i in range(GROUP):
-            a, b, c = s_v[g % 2, i, :rows], s_v[g % 2, i, rows:count], s_v[g % 2, i, count:]
-            m_a = jnp.max(halves(a, jnp.maximum), axis=1, keepdims=True)
+            if part != "second":
+                a = s_v[g % 2, i, :rows]
+                m_a = jnp.max(halves(a, jnp.maximum), axis=1, keepdims=True)
+                a = jnp.exp2(a - m_a)
+                p_v[g % 2, i, :rows] = a.astype(jnp.bfloat16)
+                l_a = jnp.sum(halves(a, jnp.add), axis=1, keepdims=True)
+                l_v[g % 2, i, :rows] = jnp.broadcast_to(1.0 / l_a, (rows, LANES))
+            b, c = s_v[g % 2, i, rows:count], s_v[g % 2, i, count:]
             m_b = jnp.max(jnp.maximum(halves(b, jnp.maximum), halves(c, jnp.maximum)), axis=1, keepdims=True)
-            a, b, c = jnp.exp2(a - m_a), jnp.exp2(b - m_b), jnp.exp2(c - m_b)
-            p_v[g % 2, i, :rows] = a.astype(jnp.bfloat16)
+            b, c = jnp.exp2(b - m_b), jnp.exp2(c - m_b)
             p_v[g % 2, i, rows:count] = b.astype(jnp.bfloat16)
             p_v[g % 2, i, count:] = c.astype(jnp.bfloat16)
-            l_a = jnp.sum(halves(a, jnp.add), axis=1, keepdims=True)
             l_b = jnp.sum(halves(b, jnp.add) + halves(c, jnp.add), axis=1, keepdims=True)
-            l_v[g % 2, i, :rows] = jnp.broadcast_to(1.0 / l_a, (rows, LANES))
             l_v[g % 2, i, rows:] = jnp.broadcast_to(1.0 / l_b, (rows, LANES))
 
-    def values(g):
+    def values(g, part):
         for i in range(GROUP):
             cols = slice((g * GROUP + i) * LANES, (g * GROUP + i + 1) * LANES)
-            o = mm(p_v[g % 2, i, :count], v_v[g * GROUP + i, 0])
-            o_a = o[:rows] * l_v[g % 2, i, :rows]
-            o_b = (o[rows:] + mm(p_v[g % 2, i, count:], v_v[g * GROUP + i, 1])) * l_v[g % 2, i, rows:]
-            o_v[:half, cols] = jnp.where(low[:half], o_a[:half], o_a[half:]).astype(jnp.bfloat16)
+            o = mm(p_v[g % 2, i, rows if part == "second" else 0:count], v_v[g * GROUP + i, 0])
+            o_b = (o[-rows:] + mm(p_v[g % 2, i, count:], v_v[g * GROUP + i, 1])) * l_v[g % 2, i, rows:]
             o_v[half:, cols] = jnp.where(low[:half], o_b[:half], o_b[half:]).astype(jnp.bfloat16)
+            if part != "second":
+                o_a = o[:rows] * l_v[g % 2, i, :rows]
+                o_v[:half, cols] = jnp.where(low[:half], o_a[:half], o_a[half:]).astype(jnp.bfloat16)
 
     def project(g):
         for c in range(width // panel):
@@ -301,18 +289,55 @@
             else:
                 y_v[:, cols] = y.astype(jnp.bfloat16)
 
-    for g in range(steps + 3):
-        if g == 3:
-            for get in get_wout:
-                get.wait()
-        if g >= 3:
-            project(g - 3)
-        if 2 <= g < steps + 2:
-            values(g - 2)
-        if 1 <= g <= steps:
-            weights(g - 1)
-        if g < steps:
-            scores(g)
+    def first_queries():
+        for p in range(pairs):
+            own = jnp.concatenate([kt_v[p, 0, :, :LANES], krt_v[0, :, :LANES]], axis=0)
+            fs_v[p] = mm(qcat[p, :rows], own) * factor + bias_v[:rows, :LANES]
+        for p in range(pairs):
+            a = fs_v[p]
+            a = jnp.exp2(a - jnp.max(a, axis=1, keepdims=True))
+            fp_v[p] = a.astype(jnp.bfloat16)
+            fl_v[p] = jnp.broadcast_to(1.0 / jnp.sum(a, axis=1, keepdims=True), (rows, LANES))
+        for p in range(pairs):
+            o = mm(fp_v[p], v_v[p, 0, :LANES]) * fl_v[p]
+            o_v[:half, p * LANES:(p + 1) * LANES] = jnp.where(low[:half], o[:half], o[half:]).astype(jnp.bfloat16)
+
+    def receive(t):
+        for d in range(2):
+            push(2 * chip_at(t) + d, me, 0).wait_recv()
+
+    even = jnp.logical_not(odd)
+    push(partner, me, 0).wait_recv()
+    pl.when(odd)(lambda: relay(1))
+    pl.when(even)(lambda: receive(1))
+    up_project([0, 1])
+    pl.when(my_chip == 0)(first_queries)
+
+    @pl.when(odd)
+    def _():
+        for t in range(2, chips):
+            relay(t)
+
+    for t in range(2, chips):
+        pl.when(even)(functools.partial(receive, t))
+        up_project([t])
+
+    def finish(part):
+        for g in range(steps + 3):
+            if g == 3:
+                for get in get_wout:
+                    get.wait()
+            if g >= 3:
+                project(g - 3)
+            if 2 <= g < steps + 2:
+                values(g - 2, part)
+            if 1 <= g <= steps:
+                weights(g - 1, part)
+            if g < steps:
+                scores(g, part)
+
+    pl.when(my_chip == 0)(functools.partial(finish, "second"))
+    pl.when(my_chip > 0)(functools.partial(finish, "both"))
     for cp in sends:
         cp.wait_send()
 
@@ -340,7 +365,7 @@
         scratch = [pltpu.VMEM(a.shape, a.dtype) for a in args]
         scratch += [
             pltpu.VMEM((n, rows + PACK_ROWS // PACKS, kv_rank), bf),
-            pltpu.VMEM((rows, kv_rank), f32),
+            pltpu.VMEM((2, rows, kv_rank), f32),
             pltpu.VMEM((rows, w_dq.shape[1]), bf),
             pltpu.VMEM((pairs, 2 * rows, LANES + rope), bf),
             pltpu.VMEM((pairs, 2, LANES, keys // 2), bf),
@@ -352,6 +377,9 @@
             pltpu.VMEM((2, GROUP, 3 * rows, keys // 2), bf),
             pltpu.VMEM((2, GROUP, 2 * rows, LANES), f32),
             pltpu.VMEM((rows, width), f32),
+            pltpu.VMEM((pairs, rows, LANES), f32),
+            pltpu.VMEM((pairs, rows, LANES), bf),
+            pltpu.VMEM((pairs, rows, LANES), f32),
             pltpu.SemaphoreType.DMA((len(args) - 2 + len(KV_CUTS) - 1 + pairs // GROUP,)),
             pltpu.SemaphoreType.DMA((n // 2 + n - 2,)),
             pltpu.SemaphoreType.DMA((n,)),

time: 14.7 us -> 14.8 us (level)
  no operation moved by 1% of the time
where the time goes in v12:
time: 14.8 us; the launch traced here: 14.7 us
  Pallas kernels  14 us (95%)
  local copies, waits for them, and re-layouts  0.73 us (5%)
    pallas_call x1, Pallas kernels, per_device(): pl.pallas_call(functools.partial(layer_kernel, n), out_shape=pltpu.VMEM(x...  14 us
    unnamed x1, local copies, waits for them, and re-layouts  0.73 us

profile of v12, /device:TPU:112, one launch (start us, length us, event | category | flops | bytes accessed | tf_op | source)
XLA Modules:
  0.0 14.7 jit_solution(9560399481295305912)
XLA Ops:
  0.0 14.0 %shard_map.118 = bf16[64,2560]{1,0:T(8,128)(2,1)S(1)} custom-call(bf16[64,2560]{1,0:T(8,128)(2,1)} %x_h.1, s32[1,64]{1,0:T(1,128)} %bitcast.3, bf16[2560,768]{1,0:T(8,128)(2,1)} %wdq_h.1, bf16[768,2560]{1,0:T(8,128)(2,1)} %wuq_h.1, bf16[768,1280]{1,0:T(8,128)(2,1)} %wqr_h.1, bf16[2560,256]{1,0:T(8,128)(2,1)} %wdkv_h.1, bf16[32,2560]{1,0:T(8,128)(2,1)} %bitcast.2, ...), custom_call_target="tpu_custom_call" | custom-call | tf_op jit(solution)/shard_map/pallas_call | solution.py:387
  14.0 0.7 %copy.14 = bf16[64,2560]{1,0:T(8,128)(2,1)} copy(bf16[64,2560]{1,0:T(8,128)(2,1)S(1)} %shard_map.118) | data formatting | bytes 655360

commit v13 on v12

--- a/solution.py
+++ b/solution.py
@@ -200,9 +200,9 @@
         for i in range(2):
             t = rope_lanes(q[:, i * LANES:(i + 1) * LANES])
             for s in range(per):
-                put_query((c * 2 + i) * per + s, slice(LANES, LANES + rope), t[:, s * rope:(s + 1) * rope])
-
-    same = iota((rope, LANES), 0) == lax.rem(iota((rope, LANES), 1), rope)
+                put_query((c * 2 + i) * per + s, slice(LANES, 2 * LANES), jnp.where(lane // rope == s, t, zero))
+
+    same = lax.rem(iota((LANES, LANES), 0), rope) == lax.rem(iota((LANES, LANES), 1), rope)
     same = jnp.where(same, 1.0, 0.0).astype(jnp.bfloat16)
 
     def up_project(slots):
@@ -358,7 +358,6 @@
         pairs = w_uq.shape[1] // LANES
         keys = n * rows
         kv_rank = w_dkv.shape[1]
-        rope = w_kr.shape[1]
         bf, f32 = jnp.bfloat16, jnp.float32
         args = (x, pos.reshape(1, rows), w_dq, w_uq, w_qr, w_dkv, w_kr.T, w_uk, w_uv, w_out,
                 gain_q, gain_kv)
@@ -367,9 +366,9 @@
             pltpu.VMEM((n, rows + PACK_ROWS // PACKS, kv_rank), bf),
             pltpu.VMEM((2, rows, kv_rank), f32),
             pltpu.VMEM((rows, w_dq.shape[1]), bf),
-            pltpu.VMEM((pairs, 2 * rows, LANES + rope), bf),
+            pltpu.VMEM((pairs, 2 * rows, 2 * LANES), bf),
             pltpu.VMEM((pairs, 2, LANES, keys // 2), bf),
-            pltpu.VMEM((2, rope, keys // 2), bf),
+            pltpu.VMEM((2, LANES, keys // 2), bf),
             pltpu.VMEM((pairs, 2, keys // 2, LANES), bf),
             pltpu.VMEM((3 * rows, keys // 2), f32),
             pltpu.VMEM((rows, w_uv.shape[1]), bf),

time: 14.8 us -> 15 us (1.014)
    pallas_call x1, Pallas kernels: 14 us -> 14.1 us  [per_device(): pl.pallas_call(functools.partial(layer_kernel, n), out_shape=pltpu.VMEM(x...]
where the time goes in v13:
time: 15 us; the launch traced here: 14.9 us
  Pallas kernels  14.1 us (94%)
  local copies, waits for them, and re-layouts  0.73 us (5%)
    pallas_call x1, Pallas kernels, per_device(): pl.pallas_call(functools.partial(layer_kernel, n), out_shape=pltpu.VMEM(x...  14.1 us
    unnamed x1, local copies, waits for them, and re-layouts  0.73 us

profile of v13, /device:TPU:112, one launch (start us, length us, event | category | flops | bytes accessed | tf_op | source)
XLA Modules:
  0.0 14.9 jit_solution(8477190444093135867)
XLA Ops:
  0.0 14.1 %shard_map.118 = bf16[64,2560]{1,0:T(8,128)(2,1)S(1)} custom-call(bf16[64,2560]{1,0:T(8,128)(2,1)} %x_h.1, s32[1,64]{1,0:T(1,128)} %bitcast.3, bf16[2560,768]{1,0:T(8,128)(2,1)} %wdq_h.1, bf16[768,2560]{1,0:T(8,128)(2,1)} %wuq_h.1, bf16[768,1280]{1,0:T(8,128)(2,1)} %wqr_h.1, bf16[2560,256]{1,0:T(8,128)(2,1)} %wdkv_h.1, bf16[32,2560]{1,0:T(8,128)(2,1)} %bitcast.2, ...), custom_call_target="tpu_custom_call" | custom-call | tf_op jit(solution)/shard_map/pallas_call | solution.py:386
  14.2 0.7 %copy.14 = bf16[64,2560]{1,0:T(8,128)(2,1)} copy(bf16[64,2560]{1,0:T(8,128)(2,1)S(1)} %shard_map.118) | data formatting | bytes 655360

commit v14 on v12

--- a/solution.py
+++ b/solution.py
@@ -291,15 +291,15 @@
 
     def first_queries():
         for p in range(pairs):
-            own = jnp.concatenate([kt_v[p, 0, :, :LANES], krt_v[0, :, :LANES]], axis=0)
-            fs_v[p] = mm(qcat[p, :rows], own) * factor + bias_v[:rows, :LANES]
+            own = jnp.concatenate([kt_v[p, 0, :, :rows], krt_v[0, :, :rows]], axis=0)
+            fs_v[p] = mm(qcat[p, :rows], own) * factor + bias_v[:rows, :rows]
         for p in range(pairs):
             a = fs_v[p]
             a = jnp.exp2(a - jnp.max(a, axis=1, keepdims=True))
             fp_v[p] = a.astype(jnp.bfloat16)
             fl_v[p] = jnp.broadcast_to(1.0 / jnp.sum(a, axis=1, keepdims=True), (rows, LANES))
         for p in range(pairs):
-            o = mm(fp_v[p], v_v[p, 0, :LANES]) * fl_v[p]
+            o = mm(fp_v[p], v_v[p, 0, :rows]) * fl_v[p]
             o_v[:half, p * LANES:(p + 1) * LANES] = jnp.where(low[:half], o[:half], o[half:]).astype(jnp.bfloat16)
 
     def receive(t):
@@ -308,15 +308,21 @@
 
     even = jnp.logical_not(odd)
     push(partner, me, 0).wait_recv()
-    pl.when(odd)(lambda: relay(1))
-    pl.when(even)(lambda: receive(1))
-    up_project([0, 1])
-    pl.when(my_chip == 0)(first_queries)
 
     @pl.when(odd)
     def _():
+        relay(1)
+        up_project([0, 1])
+        pl.when(my_chip == 0)(first_queries)
         for t in range(2, chips):
             relay(t)
+
+    @pl.when(even)
+    def _():
+        up_project([0])
+        pl.when(my_chip == 0)(first_queries)
+        receive(1)
+        up_project([1])
 
     for t in range(2, chips):
         pl.when(even)(functools.partial(receive, t))
@@ -377,8 +383,8 @@
             pltpu.VMEM((2, GROUP, 3 * rows, keys // 2), bf),
             pltpu.VMEM((2, GROUP, 2 * rows, LANES), f32),
             pltpu.VMEM((rows, width), f32),
-            pltpu.VMEM((pairs, rows, LANES), f32),
-            pltpu.VMEM((pairs, rows, LANES), bf),
+            pltpu.VMEM((pairs, rows, rows), f32),
+            pltpu.VMEM((pairs, rows, rows), bf),
             pltpu.VMEM((pairs, rows, LANES), f32),
             pltpu.SemaphoreType.DMA((len(args) - 2 + len(KV_CUTS) - 1 + pairs // GROUP,)),
             pltpu.SemaphoreType.DMA((n // 2 + n - 2,)),

time: 14.8 us -> 15 us (1.014)
  Pallas kernels: 14 us -> 14.2 us
    pallas_call x1, Pallas kernels: 14 us -> 14.2 us  [per_device(): pl.pallas_call(functools.partial(layer_kernel, n), out_shape=pltpu.VMEM(x...]
where the time goes in v14:
time: 15 us; the launch traced here: 14.9 us
  Pallas kernels  14.2 us (95%)
  local copies, waits for them, and re-layouts  0.73 us (5%)
    pallas_call x1, Pallas kernels, per_device(): pl.pallas_call(functools.partial(layer_kernel, n), out_shape=pltpu.VMEM(x...  14.2 us
    unnamed x1, local copies, waits for them, and re-layouts  0.73 us

profile of v14, /device:TPU:112, one launch (start us, length us, event | category | flops | bytes accessed | tf_op | source)
XLA Modules:
  0.0 14.9 jit_solution(17147263748655517912)
XLA Ops:
  0.0 14.2 %shard_map.118 = bf16[64,2560]{1,0:T(8,128)(2,1)S(1)} custom-call(bf16[64,2560]{1,0:T(8,128)(2,1)} %x_h.1, s32[1,64]{1,0:T(1,128)} %bitcast.3, bf16[2560,768]{1,0:T(8,128)(2,1)} %wdq_h.1, bf16[768,2560]{1,0:T(8,128)(2,1)} %wuq_h.1, bf16[768,1280]{1,0:T(8,128)(2,1)} %wqr_h.1, bf16[2560,256]{1,0:T(8,128)(2,1)} %wdkv_h.1, bf16[32,2560]{1,0:T(8,128)(2,1)} %bitcast.2, ...), custom_call_target="tpu_custom_call" | custom-call | tf_op jit(solution)/shard_map/pallas_call | solution.py:393
  14.2 0.7 %copy.14 = bf16[64,2560]{1,0:T(8,128)(2,1)} copy(bf16[64,2560]{1,0:T(8,128)(2,1)S(1)} %shard_map.118) | data formatting | bytes 655360

commit v15 on v14

--- a/solution.py
+++ b/solution.py
@@ -313,14 +313,13 @@
     def _():
         relay(1)
         up_project([0, 1])
-        pl.when(my_chip == 0)(first_queries)
         for t in range(2, chips):
             relay(t)
 
     @pl.when(even)
     def _():
         up_project([0])
-        pl.when(my_chip == 0)(first_queries)
+        pl.when(me == 0)(first_queries)
         receive(1)
         up_project([1])
 
@@ -342,8 +341,8 @@
             if g < steps:
                 scores(g, part)
 
-    pl.when(my_chip == 0)(functools.partial(finish, "second"))
-    pl.when(my_chip > 0)(functools.partial(finish, "both"))
+    pl.when(me == 0)(functools.partial(finish, "second"))
+    pl.when(me > 0)(functools.partial(finish, "both"))
     for cp in sends:
         cp.wait_send()
 

time: 15 us -> 14.7 us (0.980)
  Pallas kernels: 14.2 us -> 13.9 us
    pallas_call x1, Pallas kernels: 14.2 us -> 13.9 us  [per_device(): pl.pallas_call(functools.partial(layer_kernel, n), out_shape=pltpu.VMEM(x...]
where the time goes in v15:
time: 14.7 us; the launch traced here: 14.6 us
  Pallas kernels  13.9 us (95%)
  local copies, waits for them, and re-layouts  0.73 us (5%)
    pallas_call x1, Pallas kernels, per_device(): pl.pallas_call(functools.partial(layer_kernel, n), out_shape=pltpu.VMEM(x...  13.9 us
    unnamed x1, local copies, waits for them, and re-layouts  0.73 us

profile of v15, /device:TPU:112, one launch (start us, length us, event | category | flops | bytes accessed | tf_op | source)
XLA Modules:
  0.0 14.6 jit_solution(15886510763656134649)
XLA Ops:
  0.0 13.9 %shard_map.118 = bf16[64,2560]{1,0:T(8,128)(2,1)S(1)} custom-call(bf16[64,2560]{1,0:T(8,128)(2,1)} %x_h.1, s32[1,64]{1,0:T(1,128)} %bitcast.3, bf16[2560,768]{1,0:T(8,128)(2,1)} %wdq_h.1, bf16[768,2560]{1,0:T(8,128)(2,1)} %wuq_h.1, bf16[768,1280]{1,0:T(8,128)(2,1)} %wqr_h.1, bf16[2560,256]{1,0:T(8,128)(2,1)} %wdkv_h.1, bf16[32,2560]{1,0:T(8,128)(2,1)} %bitcast.2, ...), custom_call_target="tpu_custom_call" | custom-call | tf_op jit(solution)/shard_map/pallas_call | solution.py:392
  13.9 0.7 %copy.14 = bf16[64,2560]{1,0:T(8,128)(2,1)} copy(bf16[64,2560]{1,0:T(8,128)(2,1)S(1)} %shard_map.118) | data formatting | bytes 655360

commit v16 on v11

--- a/solution.py
+++ b/solution.py
@@ -141,9 +141,11 @@
     kr = mm(x_v[...], wkr_v[...], NT)
     for get in get_wdkv:
         get.wait()
-    for i in range(kv_rank // LANES):
-        kv_v[:, i * LANES:(i + 1) * LANES] = mm(x_v[...], wdkv_v[:, i * LANES:(i + 1) * LANES])
-    kv = kv_v[...]
+    for i in range(2):
+        at = slice(i * width // 2, (i + 1) * width // 2)
+        kv_v[i] = mm(x_v[:, at], wdkv_v[at])
+    turn = lax.rem(me, 2)
+    kv = kv_v[turn] + kv_v[1 - turn]
     get_gkv.wait()
     c_kv = rms_norm(kv, gkv_v[...].astype(jnp.float32).reshape(1, -1))
     lat[me, :rows, :] = c_kv
@@ -340,7 +342,7 @@
         scratch = [pltpu.VMEM(a.shape, a.dtype) for a in args]
         scratch += [
             pltpu.VMEM((n, rows + PACK_ROWS // PACKS, kv_rank), bf),
-            pltpu.VMEM((rows, kv_rank), f32),
+            pltpu.VMEM((2, rows, kv_rank), f32),
             pltpu.VMEM((rows, w_dq.shape[1]), bf),
             pltpu.VMEM((pairs, 2 * rows, LANES + rope), bf),
             pltpu.VMEM((pairs, 2, LANES, keys // 2), bf),

time: 14.7 us -> 14.6 us (level)
  no operation moved by 1% of the time
where the time goes in v16:
time: 14.6 us
  Pallas kernels  13.8 us (95%)
  local copies, waits for them, and re-layouts  0.73 us (5%)
    pallas_call x1, Pallas kernels, per_device(): pl.pallas_call(functools.partial(layer_kernel, n), out_shape=pltpu.VMEM(x...  13.8 us
    unnamed x1, local copies, waits for them, and re-layouts  0.73 us

profile of v16, /device:TPU:112, one launch (start us, length us, event | category | flops | bytes accessed | tf_op | source)
XLA Modules:
  0.0 14.6 jit_solution(13396760021313217679)
XLA Ops:
  0.0 13.8 %shard_map.118 = bf16[64,2560]{1,0:T(8,128)(2,1)S(1)} custom-call(bf16[64,2560]{1,0:T(8,128)(2,1)} %x_h.1, s32[1,64]{1,0:T(1,128)} %bitcast.3, bf16[2560,768]{1,0:T(8,128)(2,1)} %wdq_h.1, bf16[768,2560]{1,0:T(8,128)(2,1)} %wuq_h.1, bf16[768,1280]{1,0:T(8,128)(2,1)} %wqr_h.1, bf16[2560,256]{1,0:T(8,128)(2,1)} %wdkv_h.1, bf16[32,2560]{1,0:T(8,128)(2,1)} %bitcast.2, ...), custom_call_target="tpu_custom_call" | custom-call | tf_op jit(solution)/shard_map/pallas_call | solution.py:361
  13.8 0.7 %copy.14 = bf16[64,2560]{1,0:T(8,128)(2,1)} copy(bf16[64,2560]{1,0:T(8,128)(2,1)S(1)} %shard_map.118) | data formatting | bytes 655360
